TPU v7x, 128 devices: a whole 4x4x4 slice. The times are simulated.
128 devices in a mesh: row: 8 (over y, core), col: 16 (over x, z).
Axes of the slice: x: 4, y: 4, z: 4, core: 2. Of those that a mesh axis runs over, the one named last changes fastest.
Arguments:
- obs_cell: int32 [128, 16, 128, 128], P(('row', 'col')), may hold values from 0 to 33554431, as said below
- obs_value: bfloat16 [128, 16, 128, 128], P(('row', 'col')), may hold values from -6 to 6
- obs_weight: bfloat16 [128, 16, 128, 128], P(('row', 'col')), may hold values from 0.5 to 2
- obs_count: int32 [128, 16, 128], P(('row', 'col')), may hold values from 0 to 128, as said below
- kappa_field: float32 [4096, 8192], P('row', 'col'), may hold values from 0.2 to 6
Outputs:
- solution_field: float32 [4096, 8192], P('row', 'col')
- residual: float32 [4096, 8192], P('row', 'col')
Inputs may be any that keep to these rules, and one draw needn't show every extreme that they name: `obs_cell`: block (s, t, d) holds observations for tile t of device d, where device d is number d // 16 along row and d % (16) along col, and tile t is number t // 4 among the device's tiles along rows and t % (4) along columns, each tile 128 by 128 cells; every slot of the block, padding included, names a cell of that tile as row * 8192 + column. Slots at positions obs_count and beyond are padding. For one owner device, chosen afresh in each draw, every block from every source and tile is full.
All inputs are finite; a program needn't handle non-finite values.
Results may differ from a plain program's by a relative error of at most 0.0029.
Values may be sent and summed in bfloat16 or wider, within the bound.
A program may use at most 64 MiB of HBM per device.

v0:
```python
from functools import partial
import functools

import jax
import jax.numpy as jnp
from jax import lax
from jax.sharding import Mesh
from jax.sharding import PartitionSpec as P

TILE = 128
ITERS = 3
COL = ("col_0", "col_1")
ROW = ("row_0", "row_1")
ROW_COL = ("row_0", "row_1", "col_0", "col_1")


smooth_weight = 0.05


def split_up(x, dim, length):
    lengths = x.shape
    pieces = x.reshape(*lengths[:dim], length, lengths[dim] // length, *lengths[dim + 1 :])
    return jnp.moveaxis(pieces, dim, 0)


def laid_out(pieces, dim):
    lengths = list(pieces.shape[1:])
    lengths[dim] *= pieces.shape[0]
    return jnp.moveaxis(pieces, 0, dim).reshape(lengths)


def one_exchange(x, axis, axes, splits, concats):
    sizes = [lax.axis_size(a) for a in axes]
    pieces = split_up(x, splits[0], sizes[0])
    pieces = jnp.moveaxis(split_up(pieces, splits[1] + 1, sizes[1]), 0, 1)
    inside = pieces.shape[2:]
    pieces = pieces.reshape(-1, *inside)
    pieces = lax.all_to_all(pieces, axis, split_axis=0, concat_axis=0, tiled=True)
    pieces = laid_out(pieces.reshape(*sizes, *inside), concats[0] + 1)
    return laid_out(pieces, concats[1])


def extended(x, sides, width):
    edges = {}
    for axis, dim in sides:
        size, length = (lax.axis_size(axis), x.shape[dim])
        up = [(i, (i + 1) % size) for i in range(size - 1)]
        last = lax.slice_in_dim(x, length - width, length, axis=dim)
        leading = lax.slice_in_dim(x, 0, width, axis=dim)
        edges[dim] = (
            lax.ppermute(last, axis, up),
            lax.ppermute(leading, axis, [(b, a) for a, b in up]),
        )
    done = []
    for _, dim in sides:
        low, high = edges[dim]
        around = [(width, width) if d in done else (0, 0) for d in range(x.ndim)]
        x = jnp.concatenate([jnp.pad(low, around), x, jnp.pad(high, around)], axis=dim)
        done.append(dim)
    return x


def one_axis_at_a_time(x, axes):
    return functools.reduce(lax.psum, axes, x)


def stencil_step(padded, kappa_field):
    center = padded[1:-1, 1:-1]
    beside = padded[2:, 1:-1] + padded[:-2, 1:-1]
    beside = beside + padded[1:-1, 2:] + padded[1:-1, :-2]
    return (4.0 + kappa_field) * center - beside


def bin_tile(members, cols_all):
    cell_ids, obs_vals, obs_wts, is_live = members
    local_row = cell_ids // cols_all % TILE
    local_col = cell_ids % cols_all % TILE
    offsets = jnp.arange(TILE, dtype=jnp.int32)
    row_onehot = (local_row[:, None] == offsets[None, :]).astype(jnp.bfloat16)
    col_onehot = (local_col[:, None] == offsets[None, :]).astype(jnp.bfloat16)
    zero_fill = jnp.zeros_like(obs_wts)
    masked_weight = jnp.where(is_live, obs_wts, zero_fill)
    product = (obs_wts.astype(jnp.float32) * obs_vals.astype(jnp.float32)).astype(jnp.bfloat16)
    masked_resp = jnp.where(is_live, product, zero_fill)
    stacked = jnp.concatenate(
        [col_onehot * masked_weight[:, None], col_onehot * masked_resp[:, None]], axis=1
    )
    return lax.dot_general(
        row_onehot, stacked, (((0,), (0,)), ((), ())), preferred_element_type=jnp.float32
    )


def per_device(obs_cell, obs_value, obs_weight, obs_count, kappa_field):
    rows_dev, cols_dev = kappa_field.shape
    cols_all = cols_dev * lax.axis_size(COL)
    tiles_dev = obs_cell.shape[1]
    block_rows = obs_cell.shape[3]
    grid_shape = (1, tiles_dev, lax.axis_size(ROW), lax.axis_size(COL))
    sectioned_ids = (
        lax.all_to_all(
            lax.all_to_all(
                obs_cell.reshape(grid_shape + (block_rows,)),
                COL,
                split_axis=3,
                concat_axis=3,
                tiled=True,
            ),
            ROW,
            split_axis=2,
            concat_axis=2,
            tiled=True,
        ),
        lax.all_to_all(
            lax.all_to_all(
                obs_count.reshape(grid_shape), COL, split_axis=3, concat_axis=3, tiled=True
            ),
            ROW,
            split_axis=2,
            concat_axis=2,
            tiled=True,
        ),
    )
    sectioned_obs = (
        one_exchange(
            obs_value.reshape(grid_shape + (block_rows,)), ROW_COL, (ROW, COL), (2, 3), (2, 3)
        ),
        one_exchange(
            obs_weight.reshape(grid_shape + (block_rows,)), ROW_COL, (ROW, COL), (2, 3), (2, 3)
        ),
    )
    got_cells = sectioned_ids[0].reshape(obs_cell.shape)
    got_counts = sectioned_ids[1].reshape(obs_count.shape)
    got_values = sectioned_obs[0].reshape(obs_value.shape)
    got_weights = sectioned_obs[1].reshape(obs_weight.shape)
    flat_rows = obs_cell.shape[2] * block_rows
    positions = jnp.arange(block_rows, dtype=jnp.int32)
    is_live = (positions[None, None, :] < got_counts.reshape(tiles_dev, -1)[:, :, None]).reshape(
        tiles_dev, flat_rows
    )
    members = (
        got_cells.reshape(tiles_dev, flat_rows),
        got_values.reshape(tiles_dev, flat_rows),
        got_weights.reshape(tiles_dev, flat_rows),
        is_live,
    )
    binned = lax.map(partial(bin_tile, cols_all=cols_all), members)
    tile_rows = rows_dev // TILE
    tile_cols = cols_dev // TILE
    binned = (
        binned.reshape(tile_rows, tile_cols, TILE, 2, TILE)
        .transpose(3, 0, 2, 1, 4)
        .reshape(2, rows_dev, cols_dev)
    )
    weight_field = binned[0]
    response = binned[1]

    def operate(field):
        first = extended(field, ((ROW, 0), (COL, 1)), 1)
        inner = stencil_step(first, kappa_field)
        second = extended(inner, ((ROW, 0), (COL, 1)), 1)
        return weight_field * field + smooth_weight * stencil_step(second, kappa_field)

    solution_field = jnp.zeros_like(response)
    residual = response

    def two_products(current, image):
        return (
            one_axis_at_a_time(jnp.sum(current * current), ROW_COL),
            one_axis_at_a_time(jnp.sum(current * image), ROW_COL),
        )

    image = operate(residual)
    norm_now, curvature = two_products(residual, image)
    alpha = norm_now / curvature
    direction, along = (residual, image)
    for step in range(ITERS):
        solution_field = solution_field + alpha * direction
        residual = residual - alpha * along
        if step + 1 < ITERS:
            image = operate(residual)
            norm_next, curvature = two_products(residual, image)
            ratio = norm_next / norm_now
            alpha = norm_next / (curvature - ratio * norm_next / alpha)
            direction = residual + ratio * direction
            along = image + ratio * along
            norm_now = norm_next
    return (solution_field, residual)


def solution(mesh):
    torus = Mesh(mesh.devices.reshape(4, 2, 4, 4), ("row_0", "row_1", "col_0", "col_1"))
    placed = (
        P(ROW_COL, None, None, None),
        P(ROW_COL, None, None, None),
        P(ROW_COL, None, None, None),
        P(ROW_COL, None, None),
        P(ROW, COL),
    )
    return jax.shard_map(
        per_device,
        mesh=torus,
        in_specs=placed,
        out_specs=(P(ROW, COL), P(ROW, COL)),
        check_vma=False,
    )
```

profile of v0, /device:TPU:0, one launch (start us, length us, event | category | flops | bytes accessed | tf_op | source)
XLA Modules:
  0.0 713.8 jit_solution(13259035230895073159)
XLA Ops:
  2.3 8.0 %all-to-all-start.2 = ((s32[16,1,128]{2,1,0:T(1,128)}), s32[16,1,128]{2,1,0:T(1,128)S(1)}, u32[]{:S(2)}, u32[]{:S(2)}) async-start(s32[16,1,128]{2,1,0:T(1,128)} %reshape.169), calls=%async_computation.2 | async-start | bytes 16384 | tf_op jit(solution)/shard_map/all_to_all | solution.py:114
  10.3 7.5 %all-to-all-done.2 = s32[16,1,128]{2,1,0:T(1,128)S(1)} async-done(((s32[16,1,128]{2,1,0:T(1,128)}), s32[16,1,128]{2,1,0:T(1,128)S(1)}, u32[]{:S(2)}, u32[]{:S(2)}) %all-to-all-start.2) | async-done | bytes 8224 | tf_op jit(solution)/shard_map/all_to_all | solution.py:114
  19.9 4.5 all-to-all-start.3
  26.6 3.1 all-to-all-done.3
  29.7 4.6 all-to-all-start.4
  36.9 11.0 %all-to-all-done.4 = bf16[128,1,16,1,1,128]{5,2,4,3,1,0:T(8,128)(2,1)S(1)} async-done(((bf16[128,1,16,1,1,128]{5,2,4,3,1,0:T(8,128)(2,1)}), bf16[128,1,16,1,1,128]{5,2,4,3,1,0:T(8,128)(2,1)S(1)}, u32[]{:S(2)}, u32[]{:S(2)}) %all-to-all-start.4) | async-done | bytes 524320 | tf_op jit(solution)/shard_map/all_to_all | solution.py:38
  47.9 3.7 all-to-all-start
  52.7 16.2 %all-to-all-done = s32[1,16,8,16,128]{4,2,1,0,3:T(8,128)S(1)} async-done(((s32[1,16,8,16,128]{4,2,1,0,3:T(8,128)}), s32[1,16,8,16,128]{4,2,1,0,3:T(8,128)S(1)}, u32[]{:S(2)}, u32[]{:S(2)}) %all-to-all-start) | async-done | bytes 1048608 | tf_op jit(solution)/shard_map/all_to_all | solution.py:101
  68.9 4.7 all-to-all-start.5
  76.1 11.1 %all-to-all-done.5 = bf16[128,1,16,1,1,128]{5,2,4,3,1,0:T(8,128)(2,1)S(1)} async-done(((bf16[128,1,16,1,1,128]{5,2,4,3,1,0:T(8,128)(2,1)}), bf16[128,1,16,1,1,128]{5,2,4,3,1,0:T(8,128)(2,1)S(1)}, u32[]{:S(2)}, u32[]{:S(2)}) %all-to-all-start.5) | async-done | bytes 524320 | tf_op jit(solution)/shard_map/all_to_all | solution.py:38
  87.2 3.6 all-to-all-start.1
  92.5 14.1 %all-to-all-done.1 = s32[1,16,8,16,128]{4,3,1,0,2:T(8,128)S(1)} async-done(((s32[1,16,8,16,128]{4,3,1,0,2:T(8,128)}), s32[1,16,8,16,128]{4,3,1,0,2:T(8,128)S(1)}, u32[]{:S(2)}, u32[]{:S(2)}) %all-to-all-start.1) | async-done | bytes 1048608 | tf_op jit(solution)/shard_map/all_to_all | solution.py:100
  106.9 393.4 %while.13 = (s32[]{:T(128)}, f32[16,128,256]{2,1,0:T(8,128)}, s32[16,16384]{1,0:T(8,128)S(1)}, pred[16,16384]{1,0:T(8,128)(4,1)S(1)}, bf16[16,16384]{1,0:T(8,128...) while((s32[]{:T(128)}, f32[16,128,256]{2,1,0:T(8,128)}, s32[16,16384]{1,0:T(8,128)S(1)}, ...), condition=%wide.region_1.2_spmd, body=%wide.region_0.1_spmd.sunk | while | flops 1099677696 | bytes 17810008 | solution.py:146
  107.6 7.7 %fusion.80 = (bf16[16384,128]{1,0:T(8,128)(2,1)S(1)}, bf16[16384,128]{1,0:T(8,128)(2,1)S(1)}) fusion(s32[16384]{0:T(1024)S(1)} %get-tuple-element.236, bf16[16384]{0:T(1024)(128)(2,1)S(1)} %get-tuple-element.239, bf16[16384]{0:T(1024)(128)(2,1)S(1)} %get-tuple-element.240), kind=kLoop, calls=%fused_computation.6.clone.1 | loop fusion | flops 6291456 | bytes 8519680 | tf_op jit(solution)/shard_map/while/body/eval_jaxpr/mul | solution.py:86
  115.4 16.2 %fusion.81 = f32[16,128,256]{2,1,0:T(8,128)} fusion(f32[16,128,256]{2,1,0:T(8,128)} %get-tuple-element.252, s32[]{:T(128)} %get-tuple-element.251, bf16[16384,128]{1,0:T(8,128)(2,1)S(1)} %get-tuple-element.241, bf16[16384,128]{1,0:T(8,128)(2,1)S(1)} %get-tuple-element.242, s32[16384]{0:T(1024)S(1)} %get-tuple-element.243), kind=kOutput, calls=%fused_computation.10.clone.1 | convolution fusion | flops 1092616192 | bytes 8585728 | tf_op jit(solution)/shard_map/while/body/eval_jaxpr/dot_general | solution.py:88
  132.2 7.7 %fusion.80 = (bf16[16384,128]{1,0:T(8,128)(2,1)S(1)}, bf16[16384,128]{1,0:T(8,128)(2,1)S(1)}) fusion(s32[16384]{0:T(1024)S(1)} %get-tuple-element.236, bf16[16384]{0:T(1024)(128)(2,1)S(1)} %get-tuple-element.239, bf16[16384]{0:T(1024)(128)(2,1)S(1)} %get-tuple-element.240), kind=kLoop, calls=%fused_computation.6.clone.1 | loop fusion | flops 6291456 | bytes 8519680 | tf_op jit(solution)/shard_map/while/body/eval_jaxpr/mul | solution.py:86
  140.0 16.2 %fusion.81 = f32[16,128,256]{2,1,0:T(8,128)} fusion(f32[16,128,256]{2,1,0:T(8,128)} %get-tuple-element.252, s32[]{:T(128)} %get-tuple-element.251, bf16[16384,128]{1,0:T(8,128)(2,1)S(1)} %get-tuple-element.241, bf16[16384,128]{1,0:T(8,128)(2,1)S(1)} %get-tuple-element.242, s32[16384]{0:T(1024)S(1)} %get-tuple-element.243), kind=kOutput, calls=%fused_computation.10.clone.1 | convolution fusion | flops 1092616192 | bytes 8585728 | tf_op jit(solution)/shard_map/while/body/eval_jaxpr/dot_general | solution.py:88
  156.8 7.7 %fusion.80 = (bf16[16384,128]{1,0:T(8,128)(2,1)S(1)}, bf16[16384,128]{1,0:T(8,128)(2,1)S(1)}) fusion(s32[16384]{0:T(1024)S(1)} %get-tuple-element.236, bf16[16384]{0:T(1024)(128)(2,1)S(1)} %get-tuple-element.239, bf16[16384]{0:T(1024)(128)(2,1)S(1)} %get-tuple-element.240), kind=kLoop, calls=%fused_computation.6.clone.1 | loop fusion | flops 6291456 | bytes 8519680 | tf_op jit(solution)/shard_map/while/body/eval_jaxpr/mul | solution.py:86
  164.6 16.2 %fusion.81 = f32[16,128,256]{2,1,0:T(8,128)} fusion(f32[16,128,256]{2,1,0:T(8,128)} %get-tuple-element.252, s32[]{:T(128)} %get-tuple-element.251, bf16[16384,128]{1,0:T(8,128)(2,1)S(1)} %get-tuple-element.241, bf16[16384,128]{1,0:T(8,128)(2,1)S(1)} %get-tuple-element.242, s32[16384]{0:T(1024)S(1)} %get-tuple-element.243), kind=kOutput, calls=%fused_computation.10.clone.1 | convolution fusion | flops 1092616192 | bytes 8585728 | tf_op jit(solution)/shard_map/while/body/eval_jaxpr/dot_general | solution.py:88
  181.4 7.7 %fusion.80 = (bf16[16384,128]{1,0:T(8,128)(2,1)S(1)}, bf16[16384,128]{1,0:T(8,128)(2,1)S(1)}) fusion(s32[16384]{0:T(1024)S(1)} %get-tuple-element.236, bf16[16384]{0:T(1024)(128)(2,1)S(1)} %get-tuple-element.239, bf16[16384]{0:T(1024)(128)(2,1)S(1)} %get-tuple-element.240), kind=kLoop, calls=%fused_computation.6.clone.1 | loop fusion | flops 6291456 | bytes 8519680 | tf_op jit(solution)/shard_map/while/body/eval_jaxpr/mul | solution.py:86
  189.2 16.2 %fusion.81 = f32[16,128,256]{2,1,0:T(8,128)} fusion(f32[16,128,256]{2,1,0:T(8,128)} %get-tuple-element.252, s32[]{:T(128)} %get-tuple-element.251, bf16[16384,128]{1,0:T(8,128)(2,1)S(1)} %get-tuple-element.241, bf16[16384,128]{1,0:T(8,128)(2,1)S(1)} %get-tuple-element.242, s32[16384]{0:T(1024)S(1)} %get-tuple-element.243), kind=kOutput, calls=%fused_computation.10.clone.1 | convolution fusion | flops 1092616192 | bytes 8585728 | tf_op jit(solution)/shard_map/while/body/eval_jaxpr/dot_general | solution.py:88
  206.0 7.7 %fusion.80 = (bf16[16384,128]{1,0:T(8,128)(2,1)S(1)}, bf16[16384,128]{1,0:T(8,128)(2,1)S(1)}) fusion(s32[16384]{0:T(1024)S(1)} %get-tuple-element.236, bf16[16384]{0:T(1024)(128)(2,1)S(1)} %get-tuple-element.239, bf16[16384]{0:T(1024)(128)(2,1)S(1)} %get-tuple-element.240), kind=kLoop, calls=%fused_computation.6.clone.1 | loop fusion | flops 6291456 | bytes 8519680 | tf_op jit(solution)/shard_map/while/body/eval_jaxpr/mul | solution.py:86
  213.7 16.2 %fusion.81 = f32[16,128,256]{2,1,0:T(8,128)} fusion(f32[16,128,256]{2,1,0:T(8,128)} %get-tuple-element.252, s32[]{:T(128)} %get-tuple-element.251, bf16[16384,128]{1,0:T(8,128)(2,1)S(1)} %get-tuple-element.241, bf16[16384,128]{1,0:T(8,128)(2,1)S(1)} %get-tuple-element.242, s32[16384]{0:T(1024)S(1)} %get-tuple-element.243), kind=kOutput, calls=%fused_computation.10.clone.1 | convolution fusion | flops 1092616192 | bytes 8585728 | tf_op jit(solution)/shard_map/while/body/eval_jaxpr/dot_general | solution.py:88
  230.6 7.7 %fusion.80 = (bf16[16384,128]{1,0:T(8,128)(2,1)S(1)}, bf16[16384,128]{1,0:T(8,128)(2,1)S(1)}) fusion(s32[16384]{0:T(1024)S(1)} %get-tuple-element.236, bf16[16384]{0:T(1024)(128)(2,1)S(1)} %get-tuple-element.239, bf16[16384]{0:T(1024)(128)(2,1)S(1)} %get-tuple-element.240), kind=kLoop, calls=%fused_computation.6.clone.1 | loop fusion | flops 6291456 | bytes 8519680 | tf_op jit(solution)/shard_map/while/body/eval_jaxpr/mul | solution.py:86
  238.3 16.2 %fusion.81 = f32[16,128,256]{2,1,0:T(8,128)} fusion(f32[16,128,256]{2,1,0:T(8,128)} %get-tuple-element.252, s32[]{:T(128)} %get-tuple-element.251, bf16[16384,128]{1,0:T(8,128)(2,1)S(1)} %get-tuple-element.241, bf16[16384,128]{1,0:T(8,128)(2,1)S(1)} %get-tuple-element.242, s32[16384]{0:T(1024)S(1)} %get-tuple-element.243), kind=kOutput, calls=%fused_computation.10.clone.1 | convolution fusion | flops 1092616192 | bytes 8585728 | tf_op jit(solution)/shard_map/while/body/eval_jaxpr/dot_general | solution.py:88
  255.1 7.7 %fusion.80 = (bf16[16384,128]{1,0:T(8,128)(2,1)S(1)}, bf16[16384,128]{1,0:T(8,128)(2,1)S(1)}) fusion(s32[16384]{0:T(1024)S(1)} %get-tuple-element.236, bf16[16384]{0:T(1024)(128)(2,1)S(1)} %get-tuple-element.239, bf16[16384]{0:T(1024)(128)(2,1)S(1)} %get-tuple-element.240), kind=kLoop, calls=%fused_computation.6.clone.1 | loop fusion | flops 6291456 | bytes 8519680 | tf_op jit(solution)/shard_map/while/body/eval_jaxpr/mul | solution.py:86
  262.9 16.2 %fusion.81 = f32[16,128,256]{2,1,0:T(8,128)} fusion(f32[16,128,256]{2,1,0:T(8,128)} %get-tuple-element.252, s32[]{:T(128)} %get-tuple-element.251, bf16[16384,128]{1,0:T(8,128)(2,1)S(1)} %get-tuple-element.241, bf16[16384,128]{1,0:T(8,128)(2,1)S(1)} %get-tuple-element.242, s32[16384]{0:T(1024)S(1)} %get-tuple-element.243), kind=kOutput, calls=%fused_computation.10.clone.1 | convolution fusion | flops 1092616192 | bytes 8585728 | tf_op jit(solution)/shard_map/while/body/eval_jaxpr/dot_general | solution.py:88
  279.7 7.7 %fusion.80 = (bf16[16384,128]{1,0:T(8,128)(2,1)S(1)}, bf16[16384,128]{1,0:T(8,128)(2,1)S(1)}) fusion(s32[16384]{0:T(1024)S(1)} %get-tuple-element.236, bf16[16384]{0:T(1024)(128)(2,1)S(1)} %get-tuple-element.239, bf16[16384]{0:T(1024)(128)(2,1)S(1)} %get-tuple-element.240), kind=kLoop, calls=%fused_computation.6.clone.1 | loop fusion | flops 6291456 | bytes 8519680 | tf_op jit(solution)/shard_map/while/body/eval_jaxpr/mul | solution.py:86
  287.5 16.2 %fusion.81 = f32[16,128,256]{2,1,0:T(8,128)} fusion(f32[16,128,256]{2,1,0:T(8,128)} %get-tuple-element.252, s32[]{:T(128)} %get-tuple-element.251, bf16[16384,128]{1,0:T(8,128)(2,1)S(1)} %get-tuple-element.241, bf16[16384,128]{1,0:T(8,128)(2,1)S(1)} %get-tuple-element.242, s32[16384]{0:T(1024)S(1)} %get-tuple-element.243), kind=kOutput, calls=%fused_computation.10.clone.1 | convolution fusion | flops 1092616192 | bytes 8585728 | tf_op jit(solution)/shard_map/while/body/eval_jaxpr/dot_general | solution.py:88
  304.3 7.7 %fusion.80 = (bf16[16384,128]{1,0:T(8,128)(2,1)S(1)}, bf16[16384,128]{1,0:T(8,128)(2,1)S(1)}) fusion(s32[16384]{0:T(1024)S(1)} %get-tuple-element.236, bf16[16384]{0:T(1024)(128)(2,1)S(1)} %get-tuple-element.239, bf16[16384]{0:T(1024)(128)(2,1)S(1)} %get-tuple-element.240), kind=kLoop, calls=%fused_computation.6.clone.1 | loop fusion | flops 6291456 | bytes 8519680 | tf_op jit(solution)/shard_map/while/body/eval_jaxpr/mul | solution.py:86
  312.1 16.2 %fusion.81 = f32[16,128,256]{2,1,0:T(8,128)} fusion(f32[16,128,256]{2,1,0:T(8,128)} %get-tuple-element.252, s32[]{:T(128)} %get-tuple-element.251, bf16[16384,128]{1,0:T(8,128)(2,1)S(1)} %get-tuple-element.241, bf16[16384,128]{1,0:T(8,128)(2,1)S(1)} %get-tuple-element.242, s32[16384]{0:T(1024)S(1)} %get-tuple-element.243), kind=kOutput, calls=%fused_computation.10.clone.1 | convolution fusion | flops 1092616192 | bytes 8585728 | tf_op jit(solution)/shard_map/while/body/eval_jaxpr/dot_general | solution.py:88
  328.9 7.7 %fusion.80 = (bf16[16384,128]{1,0:T(8,128)(2,1)S(1)}, bf16[16384,128]{1,0:T(8,128)(2,1)S(1)}) fusion(s32[16384]{0:T(1024)S(1)} %get-tuple-element.236, bf16[16384]{0:T(1024)(128)(2,1)S(1)} %get-tuple-element.239, bf16[16384]{0:T(1024)(128)(2,1)S(1)} %get-tuple-element.240), kind=kLoop, calls=%fused_computation.6.clone.1 | loop fusion | flops 6291456 | bytes 8519680 | tf_op jit(solution)/shard_map/while/body/eval_jaxpr/mul | solution.py:86
  336.7 16.2 %fusion.81 = f32[16,128,256]{2,1,0:T(8,128)} fusion(f32[16,128,256]{2,1,0:T(8,128)} %get-tuple-element.252, s32[]{:T(128)} %get-tuple-element.251, bf16[16384,128]{1,0:T(8,128)(2,1)S(1)} %get-tuple-element.241, bf16[16384,128]{1,0:T(8,128)(2,1)S(1)} %get-tuple-element.242, s32[16384]{0:T(1024)S(1)} %get-tuple-element.243), kind=kOutput, calls=%fused_computation.10.clone.1 | convolution fusion | flops 1092616192 | bytes 8585728 | tf_op jit(solution)/shard_map/while/body/eval_jaxpr/dot_general | solution.py:88
  353.5 7.7 %fusion.80 = (bf16[16384,128]{1,0:T(8,128)(2,1)S(1)}, bf16[16384,128]{1,0:T(8,128)(2,1)S(1)}) fusion(s32[16384]{0:T(1024)S(1)} %get-tuple-element.236, bf16[16384]{0:T(1024)(128)(2,1)S(1)} %get-tuple-element.239, bf16[16384]{0:T(1024)(128)(2,1)S(1)} %get-tuple-element.240), kind=kLoop, calls=%fused_computation.6.clone.1 | loop fusion | flops 6291456 | bytes 8519680 | tf_op jit(solution)/shard_map/while/body/eval_jaxpr/mul | solution.py:86
  361.3 16.1 %fusion.81 = f32[16,128,256]{2,1,0:T(8,128)} fusion(f32[16,128,256]{2,1,0:T(8,128)} %get-tuple-element.252, s32[]{:T(128)} %get-tuple-element.251, bf16[16384,128]{1,0:T(8,128)(2,1)S(1)} %get-tuple-element.241, bf16[16384,128]{1,0:T(8,128)(2,1)S(1)} %get-tuple-element.242, s32[16384]{0:T(1024)S(1)} %get-tuple-element.243), kind=kOutput, calls=%fused_computation.10.clone.1 | convolution fusion | flops 1092616192 | bytes 8585728 | tf_op jit(solution)/shard_map/while/body/eval_jaxpr/dot_general | solution.py:88
  378.1 7.7 %fusion.80 = (bf16[16384,128]{1,0:T(8,128)(2,1)S(1)}, bf16[16384,128]{1,0:T(8,128)(2,1)S(1)}) fusion(s32[16384]{0:T(1024)S(1)} %get-tuple-element.236, bf16[16384]{0:T(1024)(128)(2,1)S(1)} %get-tuple-element.239, bf16[16384]{0:T(1024)(128)(2,1)S(1)} %get-tuple-element.240), kind=kLoop, calls=%fused_computation.6.clone.1 | loop fusion | flops 6291456 | bytes 8519680 | tf_op jit(solution)/shard_map/while/body/eval_jaxpr/mul | solution.py:86
  385.8 16.2 %fusion.81 = f32[16,128,256]{2,1,0:T(8,128)} fusion(f32[16,128,256]{2,1,0:T(8,128)} %get-tuple-element.252, s32[]{:T(128)} %get-tuple-element.251, bf16[16384,128]{1,0:T(8,128)(2,1)S(1)} %get-tuple-element.241, bf16[16384,128]{1,0:T(8,128)(2,1)S(1)} %get-tuple-element.242, s32[16384]{0:T(1024)S(1)} %get-tuple-element.243), kind=kOutput, calls=%fused_computation.10.clone.1 | convolution fusion | flops 1092616192 | bytes 8585728 | tf_op jit(solution)/shard_map/while/body/eval_jaxpr/dot_general | solution.py:88
  402.7 7.7 %fusion.80 = (bf16[16384,128]{1,0:T(8,128)(2,1)S(1)}, bf16[16384,128]{1,0:T(8,128)(2,1)S(1)}) fusion(s32[16384]{0:T(1024)S(1)} %get-tuple-element.236, bf16[16384]{0:T(1024)(128)(2,1)S(1)} %get-tuple-element.239, bf16[16384]{0:T(1024)(128)(2,1)S(1)} %get-tuple-element.240), kind=kLoop, calls=%fused_computation.6.clone.1 | loop fusion | flops 6291456 | bytes 8519680 | tf_op jit(solution)/shard_map/while/body/eval_jaxpr/mul | solution.py:86
  410.4 16.2 %fusion.81 = f32[16,128,256]{2,1,0:T(8,128)} fusion(f32[16,128,256]{2,1,0:T(8,128)} %get-tuple-element.252, s32[]{:T(128)} %get-tuple-element.251, bf16[16384,128]{1,0:T(8,128)(2,1)S(1)} %get-tuple-element.241, bf16[16384,128]{1,0:T(8,128)(2,1)S(1)} %get-tuple-element.242, s32[16384]{0:T(1024)S(1)} %get-tuple-element.243), kind=kOutput, calls=%fused_computation.10.clone.1 | convolution fusion | flops 1092616192 | bytes 8585728 | tf_op jit(solution)/shard_map/while/body/eval_jaxpr/dot_general | solution.py:88
  427.2 7.7 %fusion.80 = (bf16[16384,128]{1,0:T(8,128)(2,1)S(1)}, bf16[16384,128]{1,0:T(8,128)(2,1)S(1)}) fusion(s32[16384]{0:T(1024)S(1)} %get-tuple-element.236, bf16[16384]{0:T(1024)(128)(2,1)S(1)} %get-tuple-element.239, bf16[16384]{0:T(1024)(128)(2,1)S(1)} %get-tuple-element.240), kind=kLoop, calls=%fused_computation.6.clone.1 | loop fusion | flops 6291456 | bytes 8519680 | tf_op jit(solution)/shard_map/while/body/eval_jaxpr/mul | solution.py:86
  435.0 16.2 %fusion.81 = f32[16,128,256]{2,1,0:T(8,128)} fusion(f32[16,128,256]{2,1,0:T(8,128)} %get-tuple-element.252, s32[]{:T(128)} %get-tuple-element.251, bf16[16384,128]{1,0:T(8,128)(2,1)S(1)} %get-tuple-element.241, bf16[16384,128]{1,0:T(8,128)(2,1)S(1)} %get-tuple-element.242, s32[16384]{0:T(1024)S(1)} %get-tuple-element.243), kind=kOutput, calls=%fused_computation.10.clone.1 | convolution fusion | flops 1092616192 | bytes 8585728 | tf_op jit(solution)/shard_map/while/body/eval_jaxpr/dot_general | solution.py:88
  451.8 7.7 %fusion.80 = (bf16[16384,128]{1,0:T(8,128)(2,1)S(1)}, bf16[16384,128]{1,0:T(8,128)(2,1)S(1)}) fusion(s32[16384]{0:T(1024)S(1)} %get-tuple-element.236, bf16[16384]{0:T(1024)(128)(2,1)S(1)} %get-tuple-element.239, bf16[16384]{0:T(1024)(128)(2,1)S(1)} %get-tuple-element.240), kind=kLoop, calls=%fused_computation.6.clone.1 | loop fusion | flops 6291456 | bytes 8519680 | tf_op jit(solution)/shard_map/while/body/eval_jaxpr/mul | solution.py:86
  459.6 16.2 %fusion.81 = f32[16,128,256]{2,1,0:T(8,128)} fusion(f32[16,128,256]{2,1,0:T(8,128)} %get-tuple-element.252, s32[]{:T(128)} %get-tuple-element.251, bf16[16384,128]{1,0:T(8,128)(2,1)S(1)} %get-tuple-element.241, bf16[16384,128]{1,0:T(8,128)(2,1)S(1)} %get-tuple-element.242, s32[16384]{0:T(1024)S(1)} %get-tuple-element.243), kind=kOutput, calls=%fused_computation.10.clone.1 | convolution fusion | flops 1092616192 | bytes 8585728 | tf_op jit(solution)/shard_map/while/body/eval_jaxpr/dot_general | solution.py:88
  476.4 7.7 %fusion.80 = (bf16[16384,128]{1,0:T(8,128)(2,1)S(1)}, bf16[16384,128]{1,0:T(8,128)(2,1)S(1)}) fusion(s32[16384]{0:T(1024)S(1)} %get-tuple-element.236, bf16[16384]{0:T(1024)(128)(2,1)S(1)} %get-tuple-element.239, bf16[16384]{0:T(1024)(128)(2,1)S(1)} %get-tuple-element.240), kind=kLoop, calls=%fused_computation.6.clone.1 | loop fusion | flops 6291456 | bytes 8519680 | tf_op jit(solution)/shard_map/while/body/eval_jaxpr/mul | solution.py:86
  484.2 16.2 %fusion.81 = f32[16,128,256]{2,1,0:T(8,128)} fusion(f32[16,128,256]{2,1,0:T(8,128)} %get-tuple-element.252, s32[]{:T(128)} %get-tuple-element.251, bf16[16384,128]{1,0:T(8,128)(2,1)S(1)} %get-tuple-element.241, bf16[16384,128]{1,0:T(8,128)(2,1)S(1)} %get-tuple-element.242, s32[16384]{0:T(1024)S(1)} %get-tuple-element.243), kind=kOutput, calls=%fused_computation.10.clone.1 | convolution fusion | flops 1092616192 | bytes 8585728 | tf_op jit(solution)/shard_map/while/body/eval_jaxpr/dot_general | solution.py:88
  506.7 4.6 collective-permute-start.3
  518.6 5.0 collective-permute-start.7
  531.5 12.5 %all-reduce.20 = (f32[]{:T(128)}, f32[]{:T(128)}) all-reduce(f32[]{:T(128)} %get-tuple-element.162, f32[]{:T(128)} %get-tuple-element.152), channel_id=1, replica_groups=mesh['row_0'=4,'row_1'=2,'col_0'=4,'col_1'=4] {'row_0'}, use_global_device_ids=true, to_apply=%region_3.4 | all-reduce | flops 2 | bytes 16 | tf_op jit(solution)/shard_map/psum | solution.py:64
  544.0 3.1 all-reduce.23
  547.1 12.1 %all-reduce.17 = (f32[]{:T(128)}, f32[]{:T(128)}) all-reduce(f32[]{:T(128)} %get-tuple-element.148, f32[]{:T(128)} %get-tuple-element.149), channel_id=1, replica_groups=mesh['row_0'=4,'row_1'=2,'col_0'=4,'col_1'=4] {'col_0'}, use_global_device_ids=true, to_apply=%region_5.6 | all-reduce | flops 2 | bytes 16 | tf_op jit(solution)/shard_map/psum | solution.py:64
  559.2 10.0 %all-reduce.14 = (f32[]{:T(128)}, f32[]{:T(128)}) all-reduce(f32[]{:T(128)} %get-tuple-element.136, f32[]{:T(128)} %get-tuple-element.137), channel_id=1, replica_groups=mesh['row_0'=4,'row_1'=2,'col_0'=4,'col_1'=4] {'col_1'}, use_global_device_ids=true, to_apply=%region_6.7 | all-reduce | flops 2 | bytes 16 | tf_op jit(solution)/shard_map/psum | solution.py:64
  573.4 4.6 collective-permute-start.11
  585.3 4.6 collective-permute-start.15
  598.3 11.6 %all-reduce.19 = (f32[]{:T(128)}, f32[]{:T(128)}) all-reduce(f32[]{:T(128)} %get-tuple-element.113, f32[]{:T(128)} %get-tuple-element.112), channel_id=1, replica_groups=mesh['row_0'=4,'row_1'=2,'col_0'=4,'col_1'=4] {'row_0'}, use_global_device_ids=true, to_apply=%region_13.14 | all-reduce | flops 2 | bytes 16 | tf_op jit(solution)/shard_map/psum | solution.py:64
  609.9 3.2 all-reduce.22
  613.0 12.6 %all-reduce.16 = (f32[]{:T(128)}, f32[]{:T(128)}) all-reduce(f32[]{:T(128)} %get-tuple-element.146, f32[]{:T(128)} %get-tuple-element.147), channel_id=1, replica_groups=mesh['row_0'=4,'row_1'=2,'col_0'=4,'col_1'=4] {'col_0'}, use_global_device_ids=true, to_apply=%region_15.16 | all-reduce | flops 2 | bytes 16 | tf_op jit(solution)/shard_map/psum | solution.py:64
  625.6 9.5 %all-reduce.13 = (f32[]{:T(128)}, f32[]{:T(128)}) all-reduce(f32[]{:T(128)} %get-tuple-element.134, f32[]{:T(128)} %get-tuple-element.135), channel_id=1, replica_groups=mesh['row_0'=4,'row_1'=2,'col_0'=4,'col_1'=4] {'col_1'}, use_global_device_ids=true, to_apply=%region_16.17 | all-reduce | flops 2 | bytes 16 | tf_op jit(solution)/shard_map/psum | solution.py:64
  643.3 4.6 collective-permute-start.19
  655.2 4.6 collective-permute-start.23
  668.1 11.6 %all-reduce.18 = (f32[]{:T(128)}, f32[]{:T(128)}) all-reduce(f32[]{:T(128)} %get-tuple-element.111, f32[]{:T(128)} %get-tuple-element.110), channel_id=1, replica_groups=mesh['row_0'=4,'row_1'=2,'col_0'=4,'col_1'=4] {'row_0'}, use_global_device_ids=true, to_apply=%region_23.24 | all-reduce | flops 2 | bytes 16 | tf_op jit(solution)/shard_map/psum | solution.py:64
  679.7 3.1 all-reduce.21
  682.8 13.5 %all-reduce.15 = (f32[]{:T(128)}, f32[]{:T(128)}) all-reduce(f32[]{:T(128)} %get-tuple-element.144, f32[]{:T(128)} %get-tuple-element.145), channel_id=1, replica_groups=mesh['row_0'=4,'row_1'=2,'col_0'=4,'col_1'=4] {'col_0'}, use_global_device_ids=true, to_apply=%region_25.26 | all-reduce | flops 2 | bytes 16 | tf_op jit(solution)/shard_map/psum | solution.py:64
  696.3 9.3 %all-reduce.12 = (f32[]{:T(128)}, f32[]{:T(128)}) all-reduce(f32[]{:T(128)} %get-tuple-element.132, f32[]{:T(128)} %get-tuple-element.133), channel_id=1, replica_groups=mesh['row_0'=4,'row_1'=2,'col_0'=4,'col_1'=4] {'col_1'}, use_global_device_ids=true, to_apply=%region_26.27 | all-reduce | flops 2 | bytes 16 | tf_op jit(solution)/shard_map/psum | solution.py:64
  709.5 4.3 multiply_subtract_fusion
  (184 shorter events, 83.6 us)
Async XLA Ops:
  0.6 51.0 %copy-start.5 = (bf16[1,16,128,128]{3,2,1,0:T(8,128)(2,1)S(1)}, bf16[1,16,128,128]{3,2,1,0:T(8,128)(2,1)}, u32[]{:S(2)}) copy-start(bf16[1,16,128,128]{3,2,1,0:T(8,128)(2,1)} %param.8) | copy-start | bytes 1572868
  2.3 15.5 %all-to-all-start.2 = ((s32[16,1,128]{2,1,0:T(1,128)}), s32[16,1,128]{2,1,0:T(1,128)S(1)}, u32[]{:S(2)}, u32[]{:S(2)}) async-start(s32[16,1,128]{2,1,0:T(1,128)} %reshape.169), calls=%async_computation.2 | async-start | bytes 16384 | tf_op jit(solution)/shard_map/all_to_all | solution.py:114
  19.9 9.8 %all-to-all-start.3 = ((s32[8,1,256]{2,1,0:T(1,128)}), s32[8,1,256]{2,1,0:T(1,128)S(1)}, u32[]{:S(2)}, u32[]{:S(2)}) async-start(s32[8,1,256]{2,1,0:T(1,128)} %reshape.171), calls=%async_computation.3 | async-start | bytes 16384 | tf_op jit(solution)/shard_map/all_to_all | solution.py:113
  29.7 18.2 %all-to-all-start.4 = ((bf16[128,1,16,1,1,128]{5,2,4,3,1,0:T(8,128)(2,1)}), bf16[128,1,16,1,1,128]{5,2,4,3,1,0:T(8,128)(2,1)S(1)}, u32[]{:S(2)}, u32[]{:S(2)}) async-start(bf16[128,1,16,1,1,128]{5,2,4,3,1,0:T(8,128)(2,1)} %bitcast.9), calls=%async_computation.4 | async-start | bytes 1048576 | tf_op jit(solution)/shard_map/all_to_all | solution.py:38
  47.9 21.0 %all-to-all-start = ((s32[1,16,8,16,128]{4,2,1,0,3:T(8,128)}), s32[1,16,8,16,128]{4,2,1,0,3:T(8,128)S(1)}, u32[]{:S(2)}, u32[]{:S(2)}) async-start(s32[1,16,8,16,128]{4,2,1,0,3:T(8,128)} %copy.26), calls=%async_computation | async-start | bytes 2097152 | tf_op jit(solution)/shard_map/all_to_all | solution.py:101
  68.9 18.3 %all-to-all-start.5 = ((bf16[128,1,16,1,1,128]{5,2,4,3,1,0:T(8,128)(2,1)}), bf16[128,1,16,1,1,128]{5,2,4,3,1,0:T(8,128)(2,1)S(1)}, u32[]{:S(2)}, u32[]{:S(2)}) async-start(bf16[128,1,16,1,1,128]{5,2,4,3,1,0:T(8,128)(2,1)} %bitcast.18), calls=%async_computation.5 | async-start | bytes 1048576 | tf_op jit(solution)/shard_map/all_to_all | solution.py:38
  87.2 19.4 %all-to-all-start.1 = ((s32[1,16,8,16,128]{4,3,1,0,2:T(8,128)}), s32[1,16,8,16,128]{4,3,1,0,2:T(8,128)S(1)}, u32[]{:S(2)}, u32[]{:S(2)}) async-start(s32[1,16,8,16,128]{4,3,1,0,2:T(8,128)} %copy.27), calls=%async_computation.1 | async-start | bytes 2097152 | tf_op jit(solution)/shard_map/all_to_all | solution.py:100
  504.0 12.4 %copy-start = (f32[512,512]{1,0:T(8,128)S(1)}, f32[512,512]{1,0:T(8,128)}, u32[]{:S(2)}) copy-start(f32[512,512]{1,0:T(8,128)} %param.11) | copy-start | bytes 3145732
  505.2 26.3 %copy-start.2 = (f32[1,4,128,4,128]{4,3,2,1,0:T(4,128)}, f32[1,4,128,4,128]{4,3,2,1,0:T(4,128)S(1)}, u32[]{:S(2)}) copy-start(f32[1,4,128,4,128]{4,3,2,1,0:T(4,128)S(1)} %get-tuple-element.163) | copy-start | bytes 3145732
  505.4 10.2 %collective-permute-start.2 = (f32[512,1]{1,0:T(8,128)S(1)}, f32[512,1]{1,0:T(8,128)S(1)}, u32[]{:S(2)}, u32[]{:S(2)}) collective-permute-start(f32[512,1]{1,0:T(8,128)S(1)} %get-tuple-element.187), channel_id=1, source_target_pairs={{1,0},{2,1},{3,2},{4,3},{5,4},{6,5},{7,6},{8,7},{9,8},{10,9},{11,1... | collective-permute-start | bytes 6152 | tf_op jit(solution)/shard_map/ppermute | solution.py:52
  506.7 9.5 %collective-permute-start.3 = (f32[512,1]{1,0:T(8,128)S(1)}, f32[512,1]{1,0:T(8,128)S(1)}, u32[]{:S(2)}, u32[]{:S(2)}) collective-permute-start(f32[512,1]{1,0:T(8,128)S(1)} %get-tuple-element.188), channel_id=1, source_target_pairs={{0,1},{1,2},{2,3},{3,4},{4,5},{5,6},{6,7},{7,8},{8,9},{9,10},{10,1... | collective-permute-start | bytes 6152 | tf_op jit(solution)/shard_map/ppermute | solution.py:51
  511.3 5.0 collective-permute-start
  512.6 3.8 collective-permute-start.1
  517.3 10.7 %collective-permute-start.6 = (f32[512,1]{1,0:T(8,128)S(1)}, f32[512,1]{1,0:T(8,128)S(1)}, u32[]{:S(2)}, u32[]{:S(2)}) collective-permute-start(f32[512,1]{1,0:T(8,128)S(1)} %get-tuple-element.183), channel_id=1, source_target_pairs={{1,0},{2,1},{3,2},{4,3},{5,4},{6,5},{7,6},{8,7},{9,8},{10,9},{11,1... | collective-permute-start | bytes 6152 | tf_op jit(solution)/shard_map/ppermute | solution.py:52
  518.6 10.3 %collective-permute-start.7 = (f32[512,1]{1,0:T(8,128)S(1)}, f32[512,1]{1,0:T(8,128)S(1)}, u32[]{:S(2)}, u32[]{:S(2)}) collective-permute-start(f32[512,1]{1,0:T(8,128)S(1)} %get-tuple-element.184), channel_id=1, source_target_pairs={{0,1},{1,2},{2,3},{3,4},{4,5},{5,6},{6,7},{7,8},{8,9},{9,10},{10,1... | collective-permute-start | bytes 6152 | tf_op jit(solution)/shard_map/ppermute | solution.py:51
  523.7 5.3 collective-permute-start.4
  525.0 4.0 collective-permute-start.5
  570.4 25.3 %copy-start.3 = (f32[1,4,128,4,128]{4,3,2,1,0:T(4,128)S(1)}, f32[1,4,128,4,128]{4,3,2,1,0:T(4,128)}, u32[]{:S(2)}) copy-start(f32[1,4,128,4,128]{4,3,2,1,0:T(4,128)} %copy-done.2) | copy-start | bytes 3145732
  572.1 10.2 %collective-permute-start.10 = (f32[512,1]{1,0:T(8,128)S(1)}, f32[512,1]{1,0:T(8,128)S(1)}, u32[]{:S(2)}, u32[]{:S(2)}) collective-permute-start(f32[512,1]{1,0:T(8,128)S(1)} %get-tuple-element.179), channel_id=1, source_target_pairs={{1,0},{2,1},{3,2},{4,3},{5,4},{6,5},{7,6},{8,7},{9,8},{10,9},{11,1... | collective-permute-start | bytes 6152 | tf_op jit(solution)/shard_map/ppermute | solution.py:52
  573.4 8.9 %collective-permute-start.11 = (f32[512,1]{1,0:T(8,128)S(1)}, f32[512,1]{1,0:T(8,128)S(1)}, u32[]{:S(2)}, u32[]{:S(2)}) collective-permute-start(f32[512,1]{1,0:T(8,128)S(1)} %get-tuple-element.180), channel_id=1, source_target_pairs={{0,1},{1,2},{2,3},{3,4},{4,5},{5,6},{6,7},{7,8},{8,9},{9,10},{10,1... | collective-permute-start | bytes 6152 | tf_op jit(solution)/shard_map/ppermute | solution.py:51
  578.0 4.4 collective-permute-start.8
  579.3 3.8 collective-permute-start.9
  584.0 10.4 %collective-permute-start.14 = (f32[512,1]{1,0:T(8,128)S(1)}, f32[512,1]{1,0:T(8,128)S(1)}, u32[]{:S(2)}, u32[]{:S(2)}) collective-permute-start(f32[512,1]{1,0:T(8,128)S(1)} %get-tuple-element.175), channel_id=1, source_target_pairs={{1,0},{2,1},{3,2},{4,3},{5,4},{6,5},{7,6},{8,7},{9,8},{10,9},{11,1... | collective-permute-start | bytes 6152 | tf_op jit(solution)/shard_map/ppermute | solution.py:52
  585.3 10.3 %collective-permute-start.15 = (f32[512,1]{1,0:T(8,128)S(1)}, f32[512,1]{1,0:T(8,128)S(1)}, u32[]{:S(2)}, u32[]{:S(2)}) collective-permute-start(f32[512,1]{1,0:T(8,128)S(1)} %get-tuple-element.176), channel_id=1, source_target_pairs={{0,1},{1,2},{2,3},{3,4},{4,5},{5,6},{6,7},{7,8},{8,9},{9,10},{10,1... | collective-permute-start | bytes 6152 | tf_op jit(solution)/shard_map/ppermute | solution.py:51
  589.9 5.8 collective-permute-start.12
  591.2 4.5 collective-permute-start.13
  639.8 25.8 %copy-start.4 = (f32[1,4,128,4,128]{4,3,2,1,0:T(4,128)S(1)}, f32[1,4,128,4,128]{4,3,2,1,0:T(4,128)}, u32[]{:S(2)}) copy-start(f32[1,4,128,4,128]{4,3,2,1,0:T(4,128)} %copy-done.2) | copy-start | bytes 3145732
  641.8 26.3 %copy-start.1 = (f32[512,512]{1,0:T(8,128)}, f32[512,512]{1,0:T(8,128)S(1)}, u32[]{:S(2)}) copy-start(f32[512,512]{1,0:T(8,128)S(1)} %multiply_subtract_fusion.1) | copy-start | bytes 3145732
  642.0 10.2 %collective-permute-start.18 = (f32[512,1]{1,0:T(8,128)S(1)}, f32[512,1]{1,0:T(8,128)S(1)}, u32[]{:S(2)}, u32[]{:S(2)}) collective-permute-start(f32[512,1]{1,0:T(8,128)S(1)} %get-tuple-element.171), channel_id=1, source_target_pairs={{1,0},{2,1},{3,2},{4,3},{5,4},{6,5},{7,6},{8,7},{9,8},{10,9},{11,1... | collective-permute-start | bytes 6152 | tf_op jit(solution)/shard_map/ppermute | solution.py:52
  643.3 8.9 %collective-permute-start.19 = (f32[512,1]{1,0:T(8,128)S(1)}, f32[512,1]{1,0:T(8,128)S(1)}, u32[]{:S(2)}, u32[]{:S(2)}) collective-permute-start(f32[512,1]{1,0:T(8,128)S(1)} %get-tuple-element.172), channel_id=1, source_target_pairs={{0,1},{1,2},{2,3},{3,4},{4,5},{5,6},{6,7},{7,8},{8,9},{9,10},{10,1... | collective-permute-start | bytes 6152 | tf_op jit(solution)/shard_map/ppermute | solution.py:51
  647.8 4.4 collective-permute-start.16
  649.1 3.8 collective-permute-start.17
  653.9 10.4 %collective-permute-start.22 = (f32[512,1]{1,0:T(8,128)S(1)}, f32[512,1]{1,0:T(8,128)S(1)}, u32[]{:S(2)}, u32[]{:S(2)}) collective-permute-start(f32[512,1]{1,0:T(8,128)S(1)} %get-tuple-element.167), channel_id=1, source_target_pairs={{1,0},{2,1},{3,2},{4,3},{5,4},{6,5},{7,6},{8,7},{9,8},{10,9},{11,1... | collective-permute-start | bytes 6152 | tf_op jit(solution)/shard_map/ppermute | solution.py:52
  655.2 10.3 %collective-permute-start.23 = (f32[512,1]{1,0:T(8,128)S(1)}, f32[512,1]{1,0:T(8,128)S(1)}, u32[]{:S(2)}, u32[]{:S(2)}) collective-permute-start(f32[512,1]{1,0:T(8,128)S(1)} %get-tuple-element.168), channel_id=1, source_target_pairs={{0,1},{1,2},{2,3},{3,4},{4,5},{5,6},{6,7},{7,8},{8,9},{9,10},{10,1... | collective-permute-start | bytes 6152 | tf_op jit(solution)/shard_map/ppermute | solution.py:51
  659.8 5.8 collective-permute-start.20
  661.1 4.5 collective-permute-start.21
where the time goes:
time: 716 us; the launch traced here: 714 us
  matrix products  259 us (36%)
  other arithmetic  151 us (21%)
  blocking collectives  112 us (16%)
  starting transfers between devices  90.6 us (13%)
  waiting for transfers between devices  69.2 us (10%)
  local copies, waits for them, and re-layouts  20.9 us (3%)
  between operations  11.1 us (2%)
    dot_general x16, matrix products, bin_tile(): lax.dot_general(row_onehot, stacked, (((0,), (0,)), ((), ())), preferred_...  259 us
    mul x16, other arithmetic, bin_tile(): col_onehot * masked_weight[:, None]  124 us
    psum x12, blocking collectives, one_axis_at_a_time(): return functools.reduce(lax.psum, axes, x)  112 us
    ppermute x12, starting transfers between devices, extended(): lax.ppermute(last, axis, up)  46 us
    all_to_all x2, waiting for transfers between devices, one_exchange(): lax.all_to_all(pieces, axis, split_axis=0, concat_axis=0, tiled=True)  22.1 us
    all_to_all x1, waiting for transfers between devices, per_device(): lax.all_to_all(obs_cell.reshape(grid_shape + (block_rows,)), COL, split_a...  16.2 us
    ppermute x12, starting transfers between devices, extended(): lax.ppermute(leading, axis, [(b, a) for a, b in up])  15.5 us
  transfers between devices with their start and end apart: 30, of which 15 were waited for; matrix products, arithmetic and copies ran while one was open for 1% of the time, Pallas kernels for 0%

commit v1 on v0

v1 whole, which is shorter than its diff:
```python
import functools

import jax
import jax.numpy as jnp
from jax import lax
from jax.experimental import pallas as pl
from jax.experimental.pallas import tpu as pltpu
from jax.sharding import PartitionSpec as P

TILE = 128
ITERS = 3
ROW = "row"
COL = "col"
MESH = pl.DeviceIdType.MESH
BF = jnp.bfloat16
F32 = jnp.float32
PITCH = 136
STRIDE = 5

smooth_weight = 0.05


def partner(row, col, rows, cols, k):
    devices = rows * cols
    q = (row * cols + col + (k * STRIDE) % devices) % devices
    return q // cols, q % cols


def source(row, col, rows, cols, k):
    devices = rows * cols
    q = (row * cols + col + devices - (k * STRIDE) % devices) % devices
    return q // cols, q % cols


def exchange_and_bin(
    rows, cols, cell_ref, value_ref, weight_ref, count_ref, wf_ref, resp_ref,
    stage_c, stage_w, stage_p, send_c, send_v, got_c, got_v,
    low_s, w_s, p_s, high_t, sent_c, sent_v, came_c, came_v,
):
    devices = rows * cols
    tiles = cell_ref.shape[0]
    row, col = lax.axis_index(ROW), lax.axis_index(COL)
    barrier = pltpu.get_barrier_semaphore()

    def greet(k, _):
        pr, pc = partner(row, col, rows, cols, k)
        pl.semaphore_signal(barrier, inc=1, device_id=(pr, pc), device_id_type=MESH)
        return 0

    lax.fori_loop(1, devices, greet, 0)

    counts = count_ref[...].T
    slot = lax.broadcasted_iota(jnp.int32, (devices, TILE), 1)
    for t in range(tiles):
        live = slot < jnp.broadcast_to(counts[:, t : t + 1], (devices, TILE))
        cell = cell_ref[t]
        code = jnp.bitwise_and(jnp.right_shift(cell, 13 + 6), 1) * 128 + jnp.bitwise_and(cell, 127)
        code = code * 64 + jnp.bitwise_and(jnp.right_shift(cell, 13), 63)
        wide = weight_ref[t].astype(F32)
        product = (wide * value_ref[t].astype(F32)).astype(BF).astype(F32)
        stage_c[pl.ds(t * PITCH, devices), :] = code
        stage_w[pl.ds(t * PITCH, devices), :] = jnp.where(live, wide, 0.0)
        stage_p[pl.ds(t * PITCH, devices), :] = jnp.where(live, product, 0.0)

    def gather(k, _):
        pr, pc = partner(row, col, rows, cols, k)
        q = pr * cols + pc
        rows_at = pl.ds(q, tiles, stride=PITCH)
        send_c[k] = stage_c[rows_at, :].astype(jnp.int16)
        send_v[k, 0:16, :] = stage_w[rows_at, :].astype(BF)
        send_v[k, 16:32, :] = stage_p[rows_at, :].astype(BF)
        return 0

    lax.fori_loop(0, devices, gather, 0)
    pl.semaphore_wait(barrier, devices - 1)

    def send(k, _):
        pr, pc = partner(row, col, rows, cols, k)
        pltpu.make_async_remote_copy(
            send_c.at[k], got_c.at[k], sent_c, came_c.at[k // 8],
            device_id=(pr, pc), device_id_type=MESH,
        ).start()
        pltpu.make_async_remote_copy(
            send_v.at[k], got_v.at[k], sent_v, came_v.at[k // 8],
            device_id=(pr, pc), device_id_type=MESH,
        ).start()
        return 0

    lax.fori_loop(1, devices, send, 0)
    got_c[0] = send_c[0]
    got_v[0] = send_v[0]
    wf_ref[...] = jnp.zeros_like(wf_ref)
    resp_ref[...] = jnp.zeros_like(resp_ref)

    lanes = lax.broadcasted_iota(jnp.int32, (16, 128), 1).astype(F32)
    high_ids = [lanes.astype(BF), (lanes + 128.0).astype(BF)]
    subs = lax.broadcasted_iota(jnp.int32, (16, 128), 0).astype(F32)
    low_ids = [(subs + 16.0 * g).astype(BF) for g in range(4)]
    one, zero = jnp.ones((16, 128), BF), jnp.zeros((16, 128), BF)
    across = wf_ref.shape[1] // TILE

    def bin_group(g):
        code = got_c[pl.ds(g * 8, 8)].reshape(128, 128).astype(jnp.int32)
        low_s[...] = jnp.bitwise_and(code, 63).astype(F32)
        high_t[...] = jnp.right_shift(code, 6).astype(F32).T
        for s in range(8):
            w_s[pl.ds(s * 16, 16), :] = got_v[g * 8 + s, 0:16, :].astype(F32)
            p_s[pl.ds(s * 16, 16), :] = got_v[g * 8 + s, 16:32, :].astype(F32)
        for t in range(tiles):
            total = None
            for pair in range(4):
                left, right = [], []
                for s in (2 * pair, 2 * pair + 1):
                    r = s * 16 + t
                    low, w, p = (
                        jnp.broadcast_to(ref[pl.ds(r, 1), :], (16, 128)).astype(BF)
                        for ref in (low_s, w_s, p_s)
                    )
                    hits = [low == ids for ids in low_ids]
                    left.append(
                        jnp.concatenate(
                            [jnp.where(h, w, zero) for h in hits]
                            + [jnp.where(h, p, zero) for h in hits],
                            axis=0,
                        )
                    )
                    high = jnp.broadcast_to(high_t[:, r : r + 1], (128, 128)).astype(BF)
                    for v in range(8):
                        part = high[16 * v : 16 * v + 16]
                        right.append(
                            jnp.concatenate([jnp.where(part == ids, one, zero) for ids in high_ids], axis=1)
                        )
                piece = jnp.dot(
                    jnp.concatenate(left, axis=1),
                    jnp.concatenate(right, axis=0),
                    preferred_element_type=F32,
                )
                total = piece if total is None else total + piece
            for ref, at in ((wf_ref, 0), (resp_ref, 64)):
                for half in range(2):
                    where = (
                        pl.ds((t // across) * TILE + half * 64, 64),
                        pl.ds((t % across) * TILE, TILE),
                    )
                    ref[where] = ref[where] + total[at : at + 64, half * 128 : half * 128 + 128]

    def arrived(first, size, g):
        there = pl.ds(first, size)
        pltpu.make_async_copy(got_c.at[there], got_c.at[there], came_c.at[g]).wait()
        pltpu.make_async_copy(got_v.at[there], got_v.at[there], came_v.at[g]).wait()

    def step(g, _):
        @pl.when(g == 0)
        def _():
            arrived(1, 7, 0)

        @pl.when(g > 0)
        def _():
            arrived(g * 8, 8, g)

        bin_group(g)
        return 0

    lax.fori_loop(0, devices // 8, step, 0)
    out = pl.ds(1, devices - 1)
    pltpu.make_async_copy(send_c.at[out], send_c.at[out], sent_c).wait()
    pltpu.make_async_copy(send_v.at[out], send_v.at[out], sent_v).wait()


def fields(rows, cols, obs_cell, obs_value, obs_weight, obs_count, shape):
    devices = rows * cols
    tiles = obs_cell.shape[0]
    vmem = pl.BlockSpec(memory_space=pltpu.VMEM)
    stage = (tiles * PITCH, TILE)
    return pl.pallas_call(
        functools.partial(exchange_and_bin, rows, cols),
        out_shape=[jax.ShapeDtypeStruct(shape, F32)] * 2,
        in_specs=[vmem] * 4,
        out_specs=[vmem] * 2,
        scratch_shapes=[
            pltpu.VMEM(stage, jnp.int32),
            pltpu.VMEM(stage, F32),
            pltpu.VMEM(stage, F32),
            pltpu.VMEM((devices, tiles, TILE), jnp.int16),
            pltpu.VMEM((devices, 2 * tiles, TILE), BF),
            pltpu.VMEM((devices, tiles, TILE), jnp.int16),
            pltpu.VMEM((devices, 2 * tiles, TILE), BF),
            pltpu.VMEM((128, 128), F32),
            pltpu.VMEM((128, 128), F32),
            pltpu.VMEM((128, 128), F32),
            pltpu.VMEM((128, 128), F32),
            pltpu.SemaphoreType.DMA,
            pltpu.SemaphoreType.DMA,
            pltpu.SemaphoreType.DMA((devices // 8,)),
            pltpu.SemaphoreType.DMA((devices // 8,)),
        ],
        name="exchange_and_bin",
        compiler_params=pltpu.CompilerParams(collective_id=0, has_side_effects=True),
    )(obs_cell, obs_value, obs_weight, obs_count)


def extended(x, sides, width):
    edges = {}
    for axis, dim in sides:
        size, length = (lax.axis_size(axis), x.shape[dim])
        up = [(i, (i + 1) % size) for i in range(size - 1)]
        last = lax.slice_in_dim(x, length - width, length, axis=dim)
        leading = lax.slice_in_dim(x, 0, width, axis=dim)
        edges[dim] = (
            lax.ppermute(last, axis, up),
            lax.ppermute(leading, axis, [(b, a) for a, b in up]),
        )
    done = []
    for _, dim in sides:
        low, high = edges[dim]
        around = [(width, width) if d in done else (0, 0) for d in range(x.ndim)]
        x = jnp.concatenate([jnp.pad(low, around), x, jnp.pad(high, around)], axis=dim)
        done.append(dim)
    return x


def one_axis_at_a_time(x, axes):
    return functools.reduce(lax.psum, axes, x)


def stencil_step(padded, kappa_field):
    center = padded[1:-1, 1:-1]
    beside = padded[2:, 1:-1] + padded[:-2, 1:-1]
    beside = beside + padded[1:-1, 2:] + padded[1:-1, :-2]
    return (4.0 + kappa_field) * center - beside


def per_device(obs_cell, obs_value, obs_weight, obs_count, kappa_field):
    rows, cols = lax.axis_size(ROW), lax.axis_size(COL)
    weight_field, response = fields(
        rows, cols, obs_cell[0], obs_value[0], obs_weight[0], obs_count[0], kappa_field.shape
    )

    def operate(field):
        first = extended(field, ((ROW, 0), (COL, 1)), 1)
        inner = stencil_step(first, kappa_field)
        second = extended(inner, ((ROW, 0), (COL, 1)), 1)
        return weight_field * field + smooth_weight * stencil_step(second, kappa_field)

    solution_field = jnp.zeros_like(response)
    residual = response

    def two_products(current, image):
        return (
            one_axis_at_a_time(jnp.sum(current * current), (ROW, COL)),
            one_axis_at_a_time(jnp.sum(current * image), (ROW, COL)),
        )

    image = operate(residual)
    norm_now, curvature = two_products(residual, image)
    alpha = norm_now / curvature
    direction, along = (residual, image)
    for step in range(ITERS):
        solution_field = solution_field + alpha * direction
        residual = residual - alpha * along
        if step + 1 < ITERS:
            image = operate(residual)
            norm_next, curvature = two_products(residual, image)
            ratio = norm_next / norm_now
            alpha = norm_next / (curvature - ratio * norm_next / alpha)
            direction = residual + ratio * direction
            along = image + ratio * along
            norm_now = norm_next
    return (solution_field, residual)


def solution(mesh):
    placed = (
        P((ROW, COL), None, None, None),
        P((ROW, COL), None, None, None),
        P((ROW, COL), None, None, None),
        P((ROW, COL), None, None),
        P(ROW, COL),
    )
    return jax.shard_map(
        per_device,
        mesh=mesh,
        in_specs=placed,
        out_specs=(P(ROW, COL), P(ROW, COL)),
        check_vma=False,
    )
```

time: 716 us -> 341 us (0.48)
  matrix products: 259 us -> 0 us
  other arithmetic: 151 us -> 20.8 us
  Pallas kernels: 0 us -> 50.4 us
  blocking collectives: 112 us -> 162 us
  starting transfers between devices: 90.6 us -> 55 us
  waiting for transfers between devices: 69.2 us -> 37.9 us
  local copies, waits for them, and re-layouts: 20.9 us -> 2.73 us
    dot_general x16 -> x0, matrix products: 259 us -> none  [bin_tile(): lax.dot_general(row_onehot, stacked, (((0,), (0,)), ((), ())), preferred_...]
    mul x16 -> x0, other arithmetic: 124 us -> none  [bin_tile(): col_onehot * masked_weight[:, None]]
    all_to_all x6 -> x0, waiting for transfers between devices: 63 us -> none  [the longest x2 22.1 us: one_exchange(): lax.all_to_all(pieces, axis, split_axis=0, concat_axis=0, tiled=True)]
    pallas_call x0 -> x1, Pallas kernels: none -> 50.4 us  [fields(): pl.pallas_call(functools.partial(exchange_and_bin, rows, cols), out_shape...]
    psum x12 -> x6, blocking collectives: 112 us -> 162 us  [one_axis_at_a_time(): return functools.reduce(lax.psum, axes, x)]
    all_to_all x6 -> x0, starting transfers between devices: 29 us -> none  [the longest x2 9.34 us: one_exchange(): lax.all_to_all(pieces, axis, split_axis=0, concat_axis=0, tiled=True)]
    ppermute x12, waiting for transfers between devices: 0.51 us -> 28.2 us  [extended(): lax.ppermute(leading, axis, [(b, a) for a, b in up])]
  transfers between devices with their start and end apart: 30 -> 24, of which waited for: 15 -> 12; matrix products, arithmetic and copies ran while one was open for 1% -> 0% of each run, Pallas kernels for 0% -> 0%
where the time goes in v1:
time: 341 us; the launch traced here: 340 us
  blocking collectives  162 us (48%)
  starting transfers between devices  55 us (16%)
  Pallas kernels  50.4 us (15%)
  waiting for transfers between devices  37.9 us (11%)
  other arithmetic  20.8 us (6%)
  between operations  10.8 us (3%)
    psum x6, blocking collectives, one_axis_at_a_time(): return functools.reduce(lax.psum, axes, x)  162 us
    pallas_call x1, Pallas kernels, fields(): pl.pallas_call(functools.partial(exchange_and_bin, rows, cols), out_shape...  50.4 us
    ppermute x12, starting transfers between devices, extended(): lax.ppermute(last, axis, up)  39.5 us
    ppermute x12, waiting for transfers between devices, extended(): lax.ppermute(leading, axis, [(b, a) for a, b in up])  28.2 us
    ppermute x12, starting transfers between devices, extended(): lax.ppermute(leading, axis, [(b, a) for a, b in up])  15.5 us
    ppermute x12, waiting for transfers between devices, extended(): lax.ppermute(last, axis, up)  9.72 us
    reduce_sum x3, other arithmetic, two_products(): jnp.sum(current * image)  7.75 us
    sub x3, other arithmetic, per_device(): residual = residual - alpha * along  7.64 us
  transfers between devices with their start and end apart: 24, of which 12 were waited for; matrix products, arithmetic and copies ran while one was open for 0% of the time, Pallas kernels for 0%

profile of v1, /device:TPU:0, one launch (start us, length us, event | category | flops | bytes accessed | tf_op | source)
XLA Modules:
  0.0 339.8 jit_solution(12370749636260031634)
XLA Ops:
  0.6 50.4 %exchange_and_bin.1 = (f32[512,512]{1,0:T(8,128)}, f32[512,512]{1,0:T(8,128)}) custom-call(s32[16,128,128]{2,1,0:T(8,128)} %bitcast.4, bf16[16,128,128]{2,1,0:T(8,128)(2,1)} %bitcast.5, bf16[16,128,128]{2,1,0:T(8,128)(2,1)} %bitcast.6, s32[16,128]{1,0:T(8,128)} %bitcast.7), custom_call_target="tpu_custom_call" | custom-call | tf_op jit(solution)/shard_map/exchange_and_bin/pallas_call | solution.py:175
  51.1 0.0 copy-start
  51.1 0.8 fusion.56
  51.9 2.1 collective-permute-start.1
  54.0 1.3 collective-permute-start
  55.3 1.2 fusion.55
  56.5 1.3 collective-permute-start.2
  57.8 4.6 %collective-permute-start.3 = (f32[512,1]{1,0:T(8,128)S(1)}, f32[512,1]{1,0:T(8,128)S(1)}, u32[]{:S(2)}, u32[]{:S(2)}) collective-permute-start(f32[512,1]{1,0:T(8,128)S(1)} %get-tuple-element.50), channel_id=1, source_target_pairs={{0,1},{1,2},{2,3},{3,4},{4,5},{5,6},{6,7},{7,8},{8,9},{9,10},{10,1... | collective-permute-start | bytes 6152 | tf_op jit(solution)/shard_map/ppermute | solution.py:210
  62.4 0.0 collective-permute-done.1
  62.4 5.0 %collective-permute-done.2 = f32[512,1]{1,0:T(8,128)S(1)} collective-permute-done((f32[512,1]{1,0:T(8,128)S(1)}, f32[512,1]{1,0:T(8,128)S(1)}, u32[]{:S(2)}, u32[]{:S(2)}) %collective-permute-start.2) | collective-permute-done | bytes 2080 | tf_op jit(solution)/shard_map/ppermute | solution.py:211
  67.4 1.5 collective-permute-done.3
  68.9 4.0 %fusion.38 = f32[512,512]{1,0:T(8,128)S(1)} fusion(f32[512,1]{1,0:T(8,128)S(1)} %collective-permute-done.3, f32[1,512]{1,0:T(1,128)S(1)} %collective-permute-done, f32[512,512]{1,0:T(8,128)} %get-tuple-element.4, f32[1,512]{1,0:T(1,128)S(1)} %collective-permute-done.1, f32[512,1]{1,0:T(8,128)S(1)} %collective-permute-done.2, f32[512,512]{1,0:T(8,128)S(1)} %copy-done), kind=kLoop, calls=%fused_computation.79 | loop fusion | flops 5242880 | bytes 3153920 | tf_op jit(solution)/shard_map/sub | solution.py:230
  72.9 0.1 fusion.53
  73.1 2.0 collective-permute-start.5
  75.1 1.3 collective-permute-start.4
  76.4 1.3 collective-permute-start.6
  77.7 5.0 %collective-permute-start.7 = (f32[512,1]{1,0:T(8,128)S(1)}, f32[512,1]{1,0:T(8,128)S(1)}, u32[]{:S(2)}, u32[]{:S(2)}) collective-permute-start(f32[512,1]{1,0:T(8,128)S(1)} %get-tuple-element.46), channel_id=1, source_target_pairs={{0,1},{1,2},{2,3},{3,4},{4,5},{5,6},{6,7},{7,8},{8,9},{9,10},{10,1... | collective-permute-start | bytes 6152 | tf_op jit(solution)/shard_map/ppermute | solution.py:210
  82.8 0.0 collective-permute-done.4
  82.8 3.7 %collective-permute-done.6 = f32[512,1]{1,0:T(8,128)S(1)} collective-permute-done((f32[512,1]{1,0:T(8,128)S(1)}, f32[512,1]{1,0:T(8,128)S(1)}, u32[]{:S(2)}, u32[]{:S(2)}) %collective-permute-start.6) | collective-permute-done | bytes 2080 | tf_op jit(solution)/shard_map/ppermute | solution.py:211
  86.5 1.7 collective-permute-done.7
  88.2 2.6 multiply_reduce_fusion.4
  90.8 14.3 %all-reduce.17 = (f32[]{:T(128)}, f32[]{:T(128)}) all-reduce(f32[]{:T(128)} %get-tuple-element.11, f32[]{:T(128)} %get-tuple-element.10), channel_id=1, replica_groups=mesh['row'=8,'col'=16] {'row'}, use_global_device_ids=true, to_apply=%region_1.2 | all-reduce | flops 2 | bytes 16 | tf_op jit(solution)/shard_map/psum | solution.py:223
  105.2 42.8 %all-reduce.14 = (f32[]{:T(128)}, f32[]{:T(128)}) all-reduce(f32[]{:T(128)} %get-tuple-element.22, f32[]{:T(128)} %get-tuple-element.23), channel_id=1, replica_groups=mesh['row'=8,'col'=16] {'col'}, use_global_device_ids=true, to_apply=%region_2.3 | all-reduce | flops 2 | bytes 16 | tf_op jit(solution)/shard_map/psum | solution.py:223
  149.3 1.5 multiply_subtract_fusion.2
  150.8 0.1 fusion.51
  150.9 1.3 collective-permute-start.9
  152.2 1.3 collective-permute-start.8
  153.5 1.3 collective-permute-start.10
  154.8 4.6 %collective-permute-start.11 = (f32[512,1]{1,0:T(8,128)S(1)}, f32[512,1]{1,0:T(8,128)S(1)}, u32[]{:S(2)}, u32[]{:S(2)}) collective-permute-start(f32[512,1]{1,0:T(8,128)S(1)} %get-tuple-element.42), channel_id=1, source_target_pairs={{0,1},{1,2},{2,3},{3,4},{4,5},{5,6},{6,7},{7,8},{8,9},{9,10},{10,1... | collective-permute-start | bytes 6152 | tf_op jit(solution)/shard_map/ppermute | solution.py:210
  159.4 0.0 collective-permute-done.8
  159.4 5.0 %collective-permute-done.10 = f32[512,1]{1,0:T(8,128)S(1)} collective-permute-done((f32[512,1]{1,0:T(8,128)S(1)}, f32[512,1]{1,0:T(8,128)S(1)}, u32[]{:S(2)}, u32[]{:S(2)}) %collective-permute-start.10) | collective-permute-done | bytes 2080 | tf_op jit(solution)/shard_map/ppermute | solution.py:211
  164.4 1.5 collective-permute-done.11
  165.9 0.7 fusion.24
  166.7 0.1 fusion.49
  166.8 2.0 collective-permute-start.13
  168.9 1.3 collective-permute-start.12
  170.2 1.3 collective-permute-start.14
  171.5 5.0 %collective-permute-start.15 = (f32[512,1]{1,0:T(8,128)S(1)}, f32[512,1]{1,0:T(8,128)S(1)}, u32[]{:S(2)}, u32[]{:S(2)}) collective-permute-start(f32[512,1]{1,0:T(8,128)S(1)} %get-tuple-element.38), channel_id=1, source_target_pairs={{0,1},{1,2},{2,3},{3,4},{4,5},{5,6},{6,7},{7,8},{8,9},{9,10},{10,1... | collective-permute-start | bytes 6152 | tf_op jit(solution)/shard_map/ppermute | solution.py:210
  176.5 0.0 collective-permute-done.13
  176.5 4.7 %collective-permute-done.14 = f32[512,1]{1,0:T(8,128)S(1)} collective-permute-done((f32[512,1]{1,0:T(8,128)S(1)}, f32[512,1]{1,0:T(8,128)S(1)}, u32[]{:S(2)}, u32[]{:S(2)}) %collective-permute-start.14) | collective-permute-done | bytes 2080 | tf_op jit(solution)/shard_map/ppermute | solution.py:211
  181.2 1.7 collective-permute-done.15
  182.9 2.6 multiply_reduce_fusion.2
  185.5 13.5 %all-reduce.16 = (f32[]{:T(128)}, f32[]{:T(128)}) all-reduce(f32[]{:T(128)} %get-tuple-element.9, f32[]{:T(128)} %get-tuple-element.8), channel_id=1, replica_groups=mesh['row'=8,'col'=16] {'row'}, use_global_device_ids=true, to_apply=%region_7.8 | all-reduce | flops 2 | bytes 16 | tf_op jit(solution)/shard_map/psum | solution.py:223
  199.0 39.5 %all-reduce.13 = (f32[]{:T(128)}, f32[]{:T(128)}) all-reduce(f32[]{:T(128)} %get-tuple-element.20, f32[]{:T(128)} %get-tuple-element.21), channel_id=1, replica_groups=mesh['row'=8,'col'=16] {'col'}, use_global_device_ids=true, to_apply=%region_8.9 | all-reduce | flops 2 | bytes 16 | tf_op jit(solution)/shard_map/psum | solution.py:223
  243.0 1.9 multiply_subtract_fusion.1
  244.9 0.1 fusion.47
  245.0 1.3 collective-permute-start.17
  246.3 1.3 collective-permute-start.16
  247.6 1.3 collective-permute-start.18
  248.9 4.6 %collective-permute-start.19 = (f32[512,1]{1,0:T(8,128)S(1)}, f32[512,1]{1,0:T(8,128)S(1)}, u32[]{:S(2)}, u32[]{:S(2)}) collective-permute-start(f32[512,1]{1,0:T(8,128)S(1)} %get-tuple-element.34), channel_id=1, source_target_pairs={{0,1},{1,2},{2,3},{3,4},{4,5},{5,6},{6,7},{7,8},{8,9},{9,10},{10,1... | collective-permute-start | bytes 6152 | tf_op jit(solution)/shard_map/ppermute | solution.py:210
  253.5 5.0 %collective-permute-done.18 = f32[512,1]{1,0:T(8,128)S(1)} collective-permute-done((f32[512,1]{1,0:T(8,128)S(1)}, f32[512,1]{1,0:T(8,128)S(1)}, u32[]{:S(2)}, u32[]{:S(2)}) %collective-permute-start.18) | collective-permute-done | bytes 2080 | tf_op jit(solution)/shard_map/ppermute | solution.py:211
  258.5 1.5 collective-permute-done.19
  260.0 0.7 fusion.10
  260.8 0.1 fusion.45
  260.9 2.0 collective-permute-start.21
  263.0 1.3 collective-permute-start.20
  264.3 1.3 collective-permute-start.22
  265.6 5.0 %collective-permute-start.23 = (f32[512,1]{1,0:T(8,128)S(1)}, f32[512,1]{1,0:T(8,128)S(1)}, u32[]{:S(2)}, u32[]{:S(2)}) collective-permute-start(f32[512,1]{1,0:T(8,128)S(1)} %get-tuple-element.30), channel_id=1, source_target_pairs={{0,1},{1,2},{2,3},{3,4},{4,5},{5,6},{6,7},{7,8},{8,9},{9,10},{10,1... | collective-permute-start | bytes 6152 | tf_op jit(solution)/shard_map/ppermute | solution.py:210
  270.6 4.7 %collective-permute-done.22 = f32[512,1]{1,0:T(8,128)S(1)} collective-permute-done((f32[512,1]{1,0:T(8,128)S(1)}, f32[512,1]{1,0:T(8,128)S(1)}, u32[]{:S(2)}, u32[]{:S(2)}) %collective-permute-start.22) | collective-permute-done | bytes 2080 | tf_op jit(solution)/shard_map/ppermute | solution.py:211
  275.4 1.7 collective-permute-done.23
  277.1 2.6 multiply_reduce_fusion
  279.7 13.5 %all-reduce.15 = (f32[]{:T(128)}, f32[]{:T(128)}) all-reduce(f32[]{:T(128)} %get-tuple-element.7, f32[]{:T(128)} %get-tuple-element.6), channel_id=1, replica_groups=mesh['row'=8,'col'=16] {'row'}, use_global_device_ids=true, to_apply=%region_13.14 | all-reduce | flops 2 | bytes 16 | tf_op jit(solution)/shard_map/psum | solution.py:223
  293.2 38.4 %all-reduce.12 = (f32[]{:T(128)}, f32[]{:T(128)}) all-reduce(f32[]{:T(128)} %get-tuple-element.18, f32[]{:T(128)} %get-tuple-element.19), channel_id=1, replica_groups=mesh['row'=8,'col'=16] {'col'}, use_global_device_ids=true, to_apply=%region_14.15 | all-reduce | flops 2 | bytes 16 | tf_op jit(solution)/shard_map/psum | solution.py:223
  335.5 4.3 %multiply_subtract_fusion = (f32[512,512]{1,0:T(8,128)}, f32[512,512]{1,0:T(8,128)}) fusion(f32[512,512]{1,0:T(8,128)S(1)} %multiply_subtract_fusion.1, f32[512,512]{1,0:T(8,128)} %get-tuple-element.24, f32[]{:T(128)S(6)} %div.25, f32[]{:T(128)S(6)} %div.27, f32[512,512]{1,0:T(8,128)} %get-tuple-element.25, f32[512,512]{1,0:T(8,128)} %get-tuple-element.26, ...), kind=kLoop, calls=%fused_computation.92 | loop fusion | flops 3932160 | bytes 8388628 | tf_op jit(solution)/shard_map/sub | solution.py:260
  (22 shorter events, 0.1 us)
Async XLA Ops:
  51.1 17.8 %copy-start = (f32[512,512]{1,0:T(8,128)S(1)}, f32[512,512]{1,0:T(8,128)}, u32[]{:S(2)}) copy-start(f32[512,512]{1,0:T(8,128)} %param.9) | copy-start | bytes 3145732
  51.9 10.5 %collective-permute-start.1 = (f32[1,512]{1,0:T(1,128)S(1)}, f32[1,512]{1,0:T(1,128)S(1)}, u32[]{:S(2)}, u32[]{:S(2)}) collective-permute-start(f32[1,512]{1,0:T(1,128)S(1)} %get-tuple-element.51), channel_id=1, source_target_pairs={{0,16},{16,32},{32,48},{48,64},{64,80},{80,96},{96,112},{1,17},{17... | collective-permute-start | bytes 6152 | tf_op jit(solution)/shard_map/ppermute | solution.py:210
  54.0 8.3 %collective-permute-start = (f32[1,512]{1,0:T(1,128)S(1)}, f32[1,512]{1,0:T(1,128)S(1)}, u32[]{:S(2)}, u32[]{:S(2)}) collective-permute-start(f32[1,512]{1,0:T(1,128)S(1)} %get-tuple-element.52), channel_id=1, source_target_pairs={{16,0},{32,16},{48,32},{64,48},{80,64},{96,80},{112,96},{17,1},{33... | collective-permute-start | bytes 6152 | tf_op jit(solution)/shard_map/ppermute | solution.py:211
  56.5 10.9 %collective-permute-start.2 = (f32[512,1]{1,0:T(8,128)S(1)}, f32[512,1]{1,0:T(8,128)S(1)}, u32[]{:S(2)}, u32[]{:S(2)}) collective-permute-start(f32[512,1]{1,0:T(8,128)S(1)} %get-tuple-element.49), channel_id=1, source_target_pairs={{1,0},{2,1},{3,2},{4,3},{5,4},{6,5},{7,6},{8,7},{9,8},{10,9},{11,1... | collective-permute-start | bytes 6152 | tf_op jit(solution)/shard_map/ppermute | solution.py:211
  57.8 11.1 %collective-permute-start.3 = (f32[512,1]{1,0:T(8,128)S(1)}, f32[512,1]{1,0:T(8,128)S(1)}, u32[]{:S(2)}, u32[]{:S(2)}) collective-permute-start(f32[512,1]{1,0:T(8,128)S(1)} %get-tuple-element.50), channel_id=1, source_target_pairs={{0,1},{1,2},{2,3},{3,4},{4,5},{5,6},{6,7},{7,8},{8,9},{9,10},{10,1... | collective-permute-start | bytes 6152 | tf_op jit(solution)/shard_map/ppermute | solution.py:210
  68.9 19.3 %copy-start.2 = (f32[512,512]{1,0:T(8,128)S(1)}, f32[512,512]{1,0:T(8,128)}, u32[]{:S(2)}) copy-start(f32[512,512]{1,0:T(8,128)} %get-tuple-element.5) | copy-start | bytes 3145732
  72.9 15.3 %copy-start.1 = (f32[512,512]{1,0:T(8,128)S(1)}, f32[512,512]{1,0:T(8,128)}, u32[]{:S(2)}) copy-start(f32[512,512]{1,0:T(8,128)} %get-tuple-element.4) | copy-start | bytes 3145732
  73.1 9.7 %collective-permute-start.5 = (f32[1,512]{1,0:T(1,128)S(1)}, f32[1,512]{1,0:T(1,128)S(1)}, u32[]{:S(2)}, u32[]{:S(2)}) collective-permute-start(f32[1,512]{1,0:T(1,128)S(1)} %get-tuple-element.47), channel_id=1, source_target_pairs={{0,16},{16,32},{32,48},{48,64},{64,80},{80,96},{96,112},{1,17},{17... | collective-permute-start | bytes 6152 | tf_op jit(solution)/shard_map/ppermute | solution.py:210
  75.1 7.7 %collective-permute-start.4 = (f32[1,512]{1,0:T(1,128)S(1)}, f32[1,512]{1,0:T(1,128)S(1)}, u32[]{:S(2)}, u32[]{:S(2)}) collective-permute-start(f32[1,512]{1,0:T(1,128)S(1)} %get-tuple-element.48), channel_id=1, source_target_pairs={{16,0},{32,16},{48,32},{64,48},{80,64},{96,80},{112,96},{17,1},{33... | collective-permute-start | bytes 6152 | tf_op jit(solution)/shard_map/ppermute | solution.py:211
  76.4 10.1 %collective-permute-start.6 = (f32[512,1]{1,0:T(8,128)S(1)}, f32[512,1]{1,0:T(8,128)S(1)}, u32[]{:S(2)}, u32[]{:S(2)}) collective-permute-start(f32[512,1]{1,0:T(8,128)S(1)} %get-tuple-element.45), channel_id=1, source_target_pairs={{1,0},{2,1},{3,2},{4,3},{5,4},{6,5},{7,6},{8,7},{9,8},{10,9},{11,1... | collective-permute-start | bytes 6152 | tf_op jit(solution)/shard_map/ppermute | solution.py:211
  77.7 10.5 %collective-permute-start.7 = (f32[512,1]{1,0:T(8,128)S(1)}, f32[512,1]{1,0:T(8,128)S(1)}, u32[]{:S(2)}, u32[]{:S(2)}) collective-permute-start(f32[512,1]{1,0:T(8,128)S(1)} %get-tuple-element.46), channel_id=1, source_target_pairs={{0,1},{1,2},{2,3},{3,4},{4,5},{5,6},{6,7},{7,8},{8,9},{9,10},{10,1... | collective-permute-start | bytes 6152 | tf_op jit(solution)/shard_map/ppermute | solution.py:210
  150.9 8.5 %collective-permute-start.9 = (f32[1,512]{1,0:T(1,128)S(1)}, f32[1,512]{1,0:T(1,128)S(1)}, u32[]{:S(2)}, u32[]{:S(2)}) collective-permute-start(f32[1,512]{1,0:T(1,128)S(1)} %get-tuple-element.43), channel_id=1, source_target_pairs={{0,16},{16,32},{32,48},{48,64},{64,80},{80,96},{96,112},{1,17},{17... | collective-permute-start | bytes 6152 | tf_op jit(solution)/shard_map/ppermute | solution.py:210
  152.2 7.2 %collective-permute-start.8 = (f32[1,512]{1,0:T(1,128)S(1)}, f32[1,512]{1,0:T(1,128)S(1)}, u32[]{:S(2)}, u32[]{:S(2)}) collective-permute-start(f32[1,512]{1,0:T(1,128)S(1)} %get-tuple-element.44), channel_id=1, source_target_pairs={{16,0},{32,16},{48,32},{64,48},{80,64},{96,80},{112,96},{17,1},{33... | collective-permute-start | bytes 6152 | tf_op jit(solution)/shard_map/ppermute | solution.py:211
  153.5 10.9 %collective-permute-start.10 = (f32[512,1]{1,0:T(8,128)S(1)}, f32[512,1]{1,0:T(8,128)S(1)}, u32[]{:S(2)}, u32[]{:S(2)}) collective-permute-start(f32[512,1]{1,0:T(8,128)S(1)} %get-tuple-element.41), channel_id=1, source_target_pairs={{1,0},{2,1},{3,2},{4,3},{5,4},{6,5},{7,6},{8,7},{9,8},{10,9},{11,1... | collective-permute-start | bytes 6152 | tf_op jit(solution)/shard_map/ppermute | solution.py:211
  154.8 11.1 %collective-permute-start.11 = (f32[512,1]{1,0:T(8,128)S(1)}, f32[512,1]{1,0:T(8,128)S(1)}, u32[]{:S(2)}, u32[]{:S(2)}) collective-permute-start(f32[512,1]{1,0:T(8,128)S(1)} %get-tuple-element.42), channel_id=1, source_target_pairs={{0,1},{1,2},{2,3},{3,4},{4,5},{5,6},{6,7},{7,8},{8,9},{9,10},{10,1... | collective-permute-start | bytes 6152 | tf_op jit(solution)/shard_map/ppermute | solution.py:210
  166.7 16.3 %copy-start.3 = (f32[512,512]{1,0:T(8,128)S(1)}, f32[512,512]{1,0:T(8,128)}, u32[]{:S(2)}) copy-start(f32[512,512]{1,0:T(8,128)} %get-tuple-element.5) | copy-start | bytes 3145732
  166.8 9.7 %collective-permute-start.13 = (f32[1,512]{1,0:T(1,128)S(1)}, f32[1,512]{1,0:T(1,128)S(1)}, u32[]{:S(2)}, u32[]{:S(2)}) collective-permute-start(f32[1,512]{1,0:T(1,128)S(1)} %get-tuple-element.39), channel_id=1, source_target_pairs={{0,16},{16,32},{32,48},{48,64},{64,80},{80,96},{96,112},{1,17},{17... | collective-permute-start | bytes 6152 | tf_op jit(solution)/shard_map/ppermute | solution.py:210
  168.9 7.7 %collective-permute-start.12 = (f32[1,512]{1,0:T(1,128)S(1)}, f32[1,512]{1,0:T(1,128)S(1)}, u32[]{:S(2)}, u32[]{:S(2)}) collective-permute-start(f32[1,512]{1,0:T(1,128)S(1)} %get-tuple-element.40), channel_id=1, source_target_pairs={{16,0},{32,16},{48,32},{64,48},{80,64},{96,80},{112,96},{17,1},{33... | collective-permute-start | bytes 6152 | tf_op jit(solution)/shard_map/ppermute | solution.py:211
  170.2 11.0 %collective-permute-start.14 = (f32[512,1]{1,0:T(8,128)S(1)}, f32[512,1]{1,0:T(8,128)S(1)}, u32[]{:S(2)}, u32[]{:S(2)}) collective-permute-start(f32[512,1]{1,0:T(8,128)S(1)} %get-tuple-element.37), channel_id=1, source_target_pairs={{1,0},{2,1},{3,2},{4,3},{5,4},{6,5},{7,6},{8,7},{9,8},{10,9},{11,1... | collective-permute-start | bytes 6152 | tf_op jit(solution)/shard_map/ppermute | solution.py:211
  171.5 11.5 %collective-permute-start.15 = (f32[512,1]{1,0:T(8,128)S(1)}, f32[512,1]{1,0:T(8,128)S(1)}, u32[]{:S(2)}, u32[]{:S(2)}) collective-permute-start(f32[512,1]{1,0:T(8,128)S(1)} %get-tuple-element.38), channel_id=1, source_target_pairs={{0,1},{1,2},{2,3},{3,4},{4,5},{5,6},{6,7},{7,8},{8,9},{9,10},{10,1... | collective-permute-start | bytes 6152 | tf_op jit(solution)/shard_map/ppermute | solution.py:210
  245.0 8.5 %collective-permute-start.17 = (f32[1,512]{1,0:T(1,128)S(1)}, f32[1,512]{1,0:T(1,128)S(1)}, u32[]{:S(2)}, u32[]{:S(2)}) collective-permute-start(f32[1,512]{1,0:T(1,128)S(1)} %get-tuple-element.35), channel_id=1, source_target_pairs={{0,16},{16,32},{32,48},{48,64},{64,80},{80,96},{96,112},{1,17},{17... | collective-permute-start | bytes 6152 | tf_op jit(solution)/shard_map/ppermute | solution.py:210
  246.3 7.2 %collective-permute-start.16 = (f32[1,512]{1,0:T(1,128)S(1)}, f32[1,512]{1,0:T(1,128)S(1)}, u32[]{:S(2)}, u32[]{:S(2)}) collective-permute-start(f32[1,512]{1,0:T(1,128)S(1)} %get-tuple-element.36), channel_id=1, source_target_pairs={{16,0},{32,16},{48,32},{64,48},{80,64},{96,80},{112,96},{17,1},{33... | collective-permute-start | bytes 6152 | tf_op jit(solution)/shard_map/ppermute | solution.py:211
  247.6 10.9 %collective-permute-start.18 = (f32[512,1]{1,0:T(8,128)S(1)}, f32[512,1]{1,0:T(8,128)S(1)}, u32[]{:S(2)}, u32[]{:S(2)}) collective-permute-start(f32[512,1]{1,0:T(8,128)S(1)} %get-tuple-element.33), channel_id=1, source_target_pairs={{1,0},{2,1},{3,2},{4,3},{5,4},{6,5},{7,6},{8,7},{9,8},{10,9},{11,1... | collective-permute-start | bytes 6152 | tf_op jit(solution)/shard_map/ppermute | solution.py:211
  248.9 11.1 %collective-permute-start.19 = (f32[512,1]{1,0:T(8,128)S(1)}, f32[512,1]{1,0:T(8,128)S(1)}, u32[]{:S(2)}, u32[]{:S(2)}) collective-permute-start(f32[512,1]{1,0:T(8,128)S(1)} %get-tuple-element.34), channel_id=1, source_target_pairs={{0,1},{1,2},{2,3},{3,4},{4,5},{5,6},{6,7},{7,8},{8,9},{9,10},{10,1... | collective-permute-start | bytes 6152 | tf_op jit(solution)/shard_map/ppermute | solution.py:210
  260.8 16.4 %copy-start.4 = (f32[512,512]{1,0:T(8,128)S(1)}, f32[512,512]{1,0:T(8,128)}, u32[]{:S(2)}) copy-start(f32[512,512]{1,0:T(8,128)} %get-tuple-element.5) | copy-start | bytes 3145732
  260.9 9.7 %collective-permute-start.21 = (f32[1,512]{1,0:T(1,128)S(1)}, f32[1,512]{1,0:T(1,128)S(1)}, u32[]{:S(2)}, u32[]{:S(2)}) collective-permute-start(f32[1,512]{1,0:T(1,128)S(1)} %get-tuple-element.31), channel_id=1, source_target_pairs={{0,16},{16,32},{32,48},{48,64},{64,80},{80,96},{96,112},{1,17},{17... | collective-permute-start | bytes 6152 | tf_op jit(solution)/shard_map/ppermute | solution.py:210
  263.0 7.7 %collective-permute-start.20 = (f32[1,512]{1,0:T(1,128)S(1)}, f32[1,512]{1,0:T(1,128)S(1)}, u32[]{:S(2)}, u32[]{:S(2)}) collective-permute-start(f32[1,512]{1,0:T(1,128)S(1)} %get-tuple-element.32), channel_id=1, source_target_pairs={{16,0},{32,16},{48,32},{64,48},{80,64},{96,80},{112,96},{17,1},{33... | collective-permute-start | bytes 6152 | tf_op jit(solution)/shard_map/ppermute | solution.py:211
  264.3 11.1 %collective-permute-start.22 = (f32[512,1]{1,0:T(8,128)S(1)}, f32[512,1]{1,0:T(8,128)S(1)}, u32[]{:S(2)}, u32[]{:S(2)}) collective-permute-start(f32[512,1]{1,0:T(8,128)S(1)} %get-tuple-element.29), channel_id=1, source_target_pairs={{1,0},{2,1},{3,2},{4,3},{5,4},{6,5},{7,6},{8,7},{9,8},{10,9},{11,1... | collective-permute-start | bytes 6152 | tf_op jit(solution)/shard_map/ppermute | solution.py:211
  265.6 11.5 %collective-permute-start.23 = (f32[512,1]{1,0:T(8,128)S(1)}, f32[512,1]{1,0:T(8,128)S(1)}, u32[]{:S(2)}, u32[]{:S(2)}) collective-permute-start(f32[512,1]{1,0:T(8,128)S(1)} %get-tuple-element.30), channel_id=1, source_target_pairs={{0,1},{1,2},{2,3},{3,4},{4,5},{5,6},{6,7},{7,8},{8,9},{9,10},{10,1... | collective-permute-start | bytes 6152 | tf_op jit(solution)/shard_map/ppermute | solution.py:210

commit v2 on v1

--- a/solution.py
+++ b/solution.py
@@ -18,6 +18,13 @@
 STRIDE = 5
 
 smooth_weight = 0.05
+
+SCALE = 1.0 / 256.0
+SHIFT = 5.0
+GROWTH_MAX = 1000.0
+EDGE = 8
+TOP = 16
+WIDE = 128
 
 
 def partner(row, col, rows, cols, k):
@@ -167,17 +174,257 @@
     pltpu.make_async_copy(send_v.at[out], send_v.at[out], sent_v).wait()
 
 
-def fields(rows, cols, obs_cell, obs_value, obs_weight, obs_count, shape):
+def solve(m):
+    shift = SCALE * SHIFT
+
+    def at(p, i):
+        return p[i] if 0 <= i < len(p) else None
+
+    def plus(a, b):
+        return b if a is None else a if b is None else a + b
+
+    def dot(a, b):
+        total, size = None, None
+        for i, x in enumerate(a):
+            for j, y in enumerate(b):
+                term = x * y * m[i + j]
+                total, size = plus(total, term), plus(size, jnp.abs(term))
+        return total, size / jnp.abs(total)
+
+    def times_a(p):
+        out = []
+        for i in range(len(p) + 1):
+            scaled = None if at(p, i) is None else shift * p[i]
+            out.append(plus(scaled, at(p, i - 1)))
+        return out
+
+    def axpy(a, b, c):
+        return [
+            plus(at(a, i), None if at(b, i) is None else c * b[i]) for i in range(max(len(a), len(b)))
+        ]
+
+    one = jnp.ones_like(m[0])
+    x, r, p, rr, growth = [], [one], [one], m[0], one
+    for step in range(ITERS):
+        ap = times_a(p)
+        pap, grown = dot(p, ap)
+        growth = jnp.where(grown <= growth, growth, grown)
+        alpha = rr / pap
+        x, r = axpy(x, p, alpha), axpy(r, ap, -alpha)
+        if step + 1 < ITERS:
+            new, grown = dot(r, r)
+            growth = jnp.where(grown <= growth, growth, grown)
+            p, rr = axpy(r, p, new / rr), new
+    return x, r, growth
+
+
+def smooth(
+    rows, cols, kappa_ref, wf_ref, resp_ref, x_ref, r_ref, growth_ref,
+    v0, v1, v2, v3, u, w, c, send_rows, send_cols, got_rows, got_cols, got_corners,
+    part, parts, sent_edge, came_edge, sent_part, came_part,
+):
+    devices = rows * cols
+    high, wide = kappa_ref.shape
+    row, col = lax.axis_index(ROW), lax.axis_index(COL)
+    me = row * cols + col
+    above, below = (row + rows - 1) % rows, (row + 1) % rows
+    before, after = (col + cols - 1) % cols, (col + 1) % cols
+    has_above = jnp.where(row > 0, 1.0, 0.0).astype(F32)
+    has_below = jnp.where(row < rows - 1, 1.0, 0.0).astype(F32)
+    has_before = jnp.where(col > 0, 1.0, 0.0).astype(F32)
+    has_after = jnp.where(col < cols - 1, 1.0, 0.0).astype(F32)
+    tall = high + 2 * TOP
+    full = wide + WIDE
+    own_rows, own_cols = pl.ds(TOP, high), pl.ds(0, wide)
+
+    fields = (v0, w, c)
+    for ref in (v0, w, c, u, v1, v2):
+        ref[pl.ds(0, TOP), :] = jnp.zeros((TOP, full), F32)
+        ref[pl.ds(TOP + high, TOP), :] = jnp.zeros((TOP, full), F32)
+    v0[own_rows, own_cols] = resp_ref[...]
+    w[own_rows, own_cols] = (wf_ref[...] - SHIFT) * SCALE
+    c[own_rows, own_cols] = kappa_ref[...] + 4.0
+    lane = lax.broadcasted_iota(jnp.int32, (WIDE, WIDE), 1)
+    for f, ref in enumerate(fields):
+        send_rows[0, f] = ref[pl.ds(TOP, EDGE), own_cols]
+        send_rows[1, f] = ref[pl.ds(TOP + high - EDGE, EDGE), own_cols]
+        for i in range(high // WIDE):
+            block = pl.ds(TOP + i * WIDE, WIDE)
+            left = ref[block, pl.ds(0, WIDE)]
+            right = ref[block, pl.ds(wide - WIDE, WIDE)]
+            turned = jnp.where(lane < 64, left, right).T
+            send_cols[0, f, :, pl.ds(i * WIDE, WIDE)] = turned[0:EDGE]
+            send_cols[1, f, :, pl.ds(i * WIDE, WIDE)] = turned[WIDE - EDGE :]
+
+    def copies():
+        first, last = pl.ds(0, WIDE), pl.ds(high - WIDE, WIDE)
+        plan = [
+            (send_rows.at[0], got_rows.at[1], above, col),
+            (send_rows.at[1], got_rows.at[0], below, col),
+            (send_cols.at[0], got_cols.at[1], row, before),
+            (send_cols.at[1], got_cols.at[0], row, after),
+            (send_cols.at[0, :, :, first], got_corners.at[3], above, before),
+            (send_cols.at[0, :, :, last], got_corners.at[1], below, before),
+            (send_cols.at[1, :, :, first], got_corners.at[2], above, after),
+            (send_cols.at[1, :, :, last], got_corners.at[0], below, after),
+        ]
+        return [
+            pltpu.make_async_remote_copy(
+                source, target, sent_edge.at[i], came_edge.at[i], device_id=(pr, pc), device_id_type=MESH
+            )
+            for i, (source, target, pr, pc) in enumerate(plan)
+        ]
+
+    edges = copies()
+    for copy in edges:
+        copy.start()
+    for copy in edges:
+        copy.wait()
+    gap = jnp.zeros((WIDE - 2 * EDGE, WIDE), F32)
+    for f, ref in enumerate(fields):
+        keep = (has_above, has_below, has_before, has_after) if f == 0 else (1.0, 1.0, 1.0, 1.0)
+        ref[pl.ds(TOP - EDGE, EDGE), own_cols] = got_rows[0, f] * keep[0]
+        ref[pl.ds(TOP + high, EDGE), own_cols] = got_rows[1, f] * keep[1]
+
+        def turned(left, right):
+            return jnp.concatenate([right * keep[3], gap, left * keep[2]], axis=0).T
+
+        beside = pl.ds(wide, WIDE)
+        for i in range(high // WIDE):
+            at = pl.ds(i * WIDE, WIDE)
+            ref[pl.ds(TOP + i * WIDE, WIDE), beside] = turned(got_cols[0, f, :, at], got_cols[1, f, :, at])
+        upper = turned(got_corners[0, f], got_corners[1, f])
+        ref[pl.ds(TOP - EDGE, EDGE), beside] = upper[WIDE - EDGE :] * keep[0]
+        lower = turned(got_corners[2, f], got_corners[3, f])
+        ref[pl.ds(TOP + high, EDGE), beside] = lower[0:EDGE] * keep[1]
+
+    lanes = lax.broadcasted_iota(jnp.int32, (1, full), 1)
+    side = jnp.where(lanes < wide, 1.0, jnp.where(lanes < wide + 64, has_after, has_before)).astype(F32)
+
+    def laplace(ref, at, size, center):
+        tall_block = jnp.concatenate(
+            [ref[pl.ds(at - 8, 8), :], center, ref[pl.ds(at + size, 8), :]], axis=0
+        )
+        up = pltpu.roll(tall_block, 1, 0)[8 : 8 + size]
+        down = pltpu.roll(tall_block, size + 15, 0)[8 : 8 + size]
+        sideways = pltpu.roll(center, 1, 1) + pltpu.roll(center, full - 1, 1)
+        return c[pl.ds(at, size), :] * center - (up + down + sideways)
+
+    def inner(ref, at, size, mask):
+        u[pl.ds(at, size), :] = laplace(ref, at, size, ref[pl.ds(at, size), :]) * mask
+
+    def outer(ref, out, at, size, mask):
+        here = pl.ds(at, size)
+        result = w[here, :] * ref[here, :] + (smooth_weight * SCALE) * laplace(u, at, size, u[here, :])
+        out[here, :] = result * mask
+        return result
+
+    def fold(x):
+        total = x[:, 0:WIDE]
+        for i in range(1, wide // WIDE):
+            total = total + x[:, i * WIDE : (i + 1) * WIDE]
+        return total.reshape(-1, 8, WIDE).sum(axis=0)
+
+    size = 32
+    zero = jnp.zeros((8, WIDE), F32)
+    moments = []
+    for step, (ref, out) in enumerate(((v0, v1), (v1, v2), (v2, v3))):
+        inner(ref, TOP - EDGE, EDGE, side * has_above)
+        inner(ref, TOP + high, EDGE, side * has_below)
+
+        def rows_of_u(i, _, ref=ref):
+            inner(ref, pl.multiple_of(TOP + i * size, 8), size, side)
+            return 0
+
+        lax.fori_loop(0, high // size, rows_of_u, 0)
+        if step < 2:
+            outer(ref, out, TOP - EDGE, EDGE, side * has_above)
+            outer(ref, out, TOP + high, EDGE, side * has_below)
+
+        def rows_of_v(i, sums, ref=ref, out=out, step=step):
+            at = pl.multiple_of(TOP + i * size, 8)
+            new = outer(ref, out, at, size, side)[:, 0:wide]
+            old = ref[pl.ds(at, size), own_cols]
+            terms = [old * new]
+            if step == 0:
+                terms.append(old * old)
+            if step < 2:
+                terms.append(new * new)
+            return tuple(s + fold(t) for s, t in zip(sums, terms))
+
+        sums = lax.fori_loop(0, high // size, rows_of_v, (zero,) * (3, 2, 1)[step])
+        moments += [sums[1], sums[0], sums[2]] if step == 0 else list(sums)
+
+    column = lax.broadcasted_iota(jnp.int32, (1, WIDE), 1)
+    mine = jnp.zeros((1, WIDE), F32)
+    for j, m in enumerate(moments):
+        mine = mine + jnp.where(column == j, jnp.sum(jnp.sum(m, axis=0, keepdims=True), axis=1, keepdims=True), 0.0)
+    part[...] = mine
+    parts[me] = mine
+
+    def tell(k, _):
+        pr, pc = partner(row, col, rows, cols, k)
+        pltpu.make_async_remote_copy(
+            part, parts.at[me], sent_part, came_part, device_id=(pr, pc), device_id_type=MESH
+        ).start()
+        return 0
+
+    lax.fori_loop(1, devices, tell, 0)
+    others = pl.ds(1, devices - 1)
+    pltpu.make_async_copy(parts.at[others], parts.at[others], came_part).wait()
+    total = jnp.sum(parts[...], axis=0)
+    m = [jnp.sum(jnp.where(column == j, total, 0.0), axis=1, keepdims=True) for j in range(len(moments))]
+    xs, rs, growth = solve([jnp.broadcast_to(value, (1, WIDE)) for value in m])
+    growth_ref[...] = growth
+
+    def combine(i, _):
+        at = pl.ds(pl.multiple_of(i * size, 8), size)
+        held = pl.ds(pl.multiple_of(TOP + i * size, 8), size)
+
+        def spread(value):
+            return jnp.concatenate([jnp.broadcast_to(value, (size, WIDE))] * (wide // WIDE), axis=1)
+
+        basis = [ref[held, own_cols] for ref in (v0, v1, v2, v3)]
+        x_ref[at, :] = sum(spread(k * SCALE) * v for k, v in zip(xs, basis))
+        r_ref[at, :] = sum(spread(k) * v for k, v in zip(rs, basis))
+        return 0
+
+    lax.fori_loop(0, high // size, combine, 0)
+    pltpu.make_async_copy(parts.at[others], parts.at[others], sent_part).wait()
+
+
+def whole(rows, cols, cell, value, weight, count, kappa, x, r, growth, wf_out, resp_out, wf, resp, *rest):
+    first, second, keep = rest[:15], rest[15:-1], rest[-1]
+    exchange_and_bin(rows, cols, cell, value, weight, count, wf, resp, *first)
+    kept = [
+        pltpu.make_async_copy(wf, wf_out, keep.at[0]),
+        pltpu.make_async_copy(resp, resp_out, keep.at[1]),
+    ]
+    for copy in kept:
+        copy.start()
+    smooth(rows, cols, kappa, wf, resp, x, r, growth, *second)
+    for copy in kept:
+        copy.wait()
+
+
+def run(rows, cols, obs_cell, obs_value, obs_weight, obs_count, kappa_field):
     devices = rows * cols
     tiles = obs_cell.shape[0]
+    high, wide = kappa_field.shape
     vmem = pl.BlockSpec(memory_space=pltpu.VMEM)
+    anywhere = pl.BlockSpec(memory_space=pl.ANY)
     stage = (tiles * PITCH, TILE)
+    work = pltpu.VMEM((high + 2 * TOP, wide + WIDE), F32)
+    dma = pltpu.SemaphoreType.DMA
+    shape = jax.ShapeDtypeStruct((high, wide), F32)
     return pl.pallas_call(
-        functools.partial(exchange_and_bin, rows, cols),
-        out_shape=[jax.ShapeDtypeStruct(shape, F32)] * 2,
-        in_specs=[vmem] * 4,
-        out_specs=[vmem] * 2,
+        functools.partial(whole, rows, cols),
+        out_shape=[shape, shape, jax.ShapeDtypeStruct((1, WIDE), F32), shape, shape],
+        in_specs=[vmem] * 5,
+        out_specs=[vmem] * 3 + [anywhere] * 2,
         scratch_shapes=[
+            pltpu.VMEM((high, wide), F32),
+            pltpu.VMEM((high, wide), F32),
             pltpu.VMEM(stage, jnp.int32),
             pltpu.VMEM(stage, F32),
             pltpu.VMEM(stage, F32),
@@ -189,14 +436,27 @@
             pltpu.VMEM((128, 128), F32),
             pltpu.VMEM((128, 128), F32),
             pltpu.VMEM((128, 128), F32),
-            pltpu.SemaphoreType.DMA,
-            pltpu.SemaphoreType.DMA,
-            pltpu.SemaphoreType.DMA((devices // 8,)),
-            pltpu.SemaphoreType.DMA((devices // 8,)),
+            dma,
+            dma,
+            dma((devices // 8,)),
+            dma((devices // 8,)),
+            *[work] * 7,
+            pltpu.VMEM((2, 3, EDGE, wide), F32),
+            pltpu.VMEM((2, 3, EDGE, high), F32),
+            pltpu.VMEM((2, 3, EDGE, wide), F32),
+            pltpu.VMEM((2, 3, EDGE, high), F32),
+            pltpu.VMEM((4, 3, EDGE, WIDE), F32),
+            pltpu.VMEM((1, WIDE), F32),
+            pltpu.VMEM((devices, 1, WIDE), F32),
+            dma((8,)),
+            dma((8,)),
+            dma,
+            dma,
+            dma((2,)),
         ],
-        name="exchange_and_bin",
+        name="bin_and_smooth",
         compiler_params=pltpu.CompilerParams(collective_id=0, has_side_effects=True),
-    )(obs_cell, obs_value, obs_weight, obs_count)
+    )(obs_cell, obs_value, obs_weight, obs_count, kappa_field)
 
 
 def extended(x, sides, width):
@@ -230,12 +490,7 @@
     return (4.0 + kappa_field) * center - beside
 
 
-def per_device(obs_cell, obs_value, obs_weight, obs_count, kappa_field):
-    rows, cols = lax.axis_size(ROW), lax.axis_size(COL)
-    weight_field, response = fields(
-        rows, cols, obs_cell[0], obs_value[0], obs_weight[0], obs_count[0], kappa_field.shape
-    )
-
+def step_by_step(weight_field, response, kappa_field):
     def operate(field):
         first = extended(field, ((ROW, 0), (COL, 1)), 1)
         inner = stencil_step(first, kappa_field)
@@ -269,6 +524,19 @@
     return (solution_field, residual)
 
 
+def per_device(obs_cell, obs_value, obs_weight, obs_count, kappa_field):
+    rows, cols = lax.axis_size(ROW), lax.axis_size(COL)
+    x, r, growth, weight_field, response = run(
+        rows, cols, obs_cell[0], obs_value[0], obs_weight[0], obs_count[0], kappa_field
+    )
+    return lax.cond(
+        growth[0, 0] <= GROWTH_MAX,
+        lambda x, r, *rest: (x, r),
+        lambda x, r, *rest: step_by_step(*rest),
+        x, r, weight_field, response, kappa_field,
+    )
+
+
 def solution(mesh):
     placed = (
         P((ROW, COL), None, None, None),

time: 341 us -> 85.3 us (0.25)
  blocking collectives: 162 us -> 0 us
  starting transfers between devices: 55 us -> 0 us
  waiting for transfers between devices: 37.9 us -> 0 us
  Pallas kernels: 50.4 us -> 79.9 us
  other arithmetic: 20.8 us -> 0 us
  between operations: 10.8 us -> 0.72 us
    psum x6 -> x0, blocking collectives: 162 us -> none  [one_axis_at_a_time(): return functools.reduce(lax.psum, axes, x)]
    ppermute x24 -> x0, starting transfers between devices: 55 us -> none  [the longest x12 39.5 us: extended(): lax.ppermute(last, axis, up)]
    ppermute x24 -> x0, waiting for transfers between devices: 37.9 us -> none  [the longest x12 28.2 us: extended(): lax.ppermute(leading, axis, [(b, a) for a, b in up])]
    pallas_call x1, Pallas kernels: 50.4 us -> 79.9 us  [run(): pl.pallas_call(functools.partial(whole, rows, cols), out_shape=[shape, sh...]
    sub x6 -> x0, other arithmetic: 13.1 us -> none  [the longest x3 7.64 us: per_device(): residual = residual - alpha * along]
    reduce_sum x3 -> x0, other arithmetic: 7.75 us -> none  [two_products(): jnp.sum(current * image)]
    unnamed x10 -> x8, local copies, waits for them, and re-layouts: 0.02 us -> 3.99 us
  transfers between devices with their start and end apart: 24 -> 0, of which waited for: 12 -> 0; matrix products, arithmetic and copies ran while one was open for 0% -> 0% of each run, Pallas kernels for 0% -> 0%
where the time goes in v2:
time: 85.3 us; the launch traced here: 84.8 us
  Pallas kernels  79.9 us (94%)
  local copies, waits for them, and re-layouts  3.99 us (5%)
    pallas_call x1, Pallas kernels, run(): pl.pallas_call(functools.partial(whole, rows, cols), out_shape=[shape, sh...  79.9 us
    unnamed x8, local copies, waits for them, and re-layouts  3.99 us

profile of v2, /device:TPU:0, one launch (start us, length us, event | category | flops | bytes accessed | tf_op | source)
XLA Modules:
  0.0 84.8 jit_solution(2474800344474822666)
XLA Ops:
  0.6 0.0 copy-start
  0.6 79.9 %bin_and_smooth.1 = (f32[512,512]{1,0:T(8,128)}, f32[512,512]{1,0:T(8,128)}, f32[1,128]{1,0:T(1,128)}, f32[512,512]{1,0:T(8,128)S(1)}, f32[512,512]{1,0:T(8,128)S(1)}) custom-call(s32[16,128,128]{2,1,0:T(8,128)} %bitcast.6, bf16[16,128,128]{2,1,0:T(8,128)(2,1)} %bitcast.7, bf16[16,128,128]{2,1,0:T(8,128)(2,1)} %bitcast.8, s32[16,128]{1,0:T(8,128)} %bitcast.9, ...), custom_call_target="tpu_custom_call" | custom-call | tf_op jit(solution)/shard_map/bin_and_smooth/pallas_call | solution.py:420
  80.5 0.0 copy-start.6
  80.6 0.7 copy-done.6
  81.3 0.0 copy-done
  81.3 0.2 conditional.1
  81.5 0.0 copy-start.5
  81.5 2.4 %copy.17 = f32[512,512]{1,0:T(8,128)} copy(f32[512,512]{1,0:T(8,128)} %get-tuple-element.82) | data formatting | bytes 2097152
  83.9 0.0 copy-done.5
  83.9 1.0 %copy.18 = f32[512,512]{1,0:T(8,128)} copy(f32[512,512]{1,0:T(8,128)S(1)} %copy-done.5) | data formatting | bytes 2097152
Async XLA Ops:
  0.6 80.6 %copy-start = (f32[512,512]{1,0:T(8,128)S(1)}, f32[512,512]{1,0:T(8,128)}, u32[]{:S(2)}) copy-start(f32[512,512]{1,0:T(8,128)} %kappa.1) | copy-start | bytes 3145732
  80.5 0.7 copy-start.6
  81.5 2.4 %copy-start.5 = (f32[512,512]{1,0:T(8,128)S(1)}, f32[512,512]{1,0:T(8,128)}, u32[]{:S(2)}) copy-start(f32[512,512]{1,0:T(8,128)} %get-tuple-element.83) | copy-start | bytes 3145732

commit v3 on v2

--- a/solution.py
+++ b/solution.py
@@ -12,6 +12,7 @@
 ROW = "row"
 COL = "col"
 MESH = pl.DeviceIdType.MESH
+LOGICAL = pl.DeviceIdType.LOGICAL
 BF = jnp.bfloat16
 F32 = jnp.float32
 PITCH = 136
@@ -27,34 +28,40 @@
 WIDE = 128
 
 
-def partner(row, col, rows, cols, k):
-    devices = rows * cols
-    q = (row * cols + col + (k * STRIDE) % devices) % devices
-    return q // cols, q % cols
-
-
-def source(row, col, rows, cols, k):
-    devices = rows * cols
-    q = (row * cols + col + devices - (k * STRIDE) % devices) % devices
-    return q // cols, q % cols
+def partner(me, devices, k):
+    return lax.rem(me + STRIDE * k, devices)
+
+
+def each_partner(devices, act):
+    for k in range(1, 8):
+        act(k)
+
+    def some(g, _):
+        for k in range(8):
+            act(g * 8 + k)
+        return 0
+
+    lax.fori_loop(1, devices // 8, some, 0)
 
 
 def exchange_and_bin(
-    rows, cols, cell_ref, value_ref, weight_ref, count_ref, wf_ref, resp_ref,
+    rows, cols, loads, cell_ref, value_ref, weight_ref, count_ref, wf_ref, resp_ref,
     stage_c, stage_w, stage_p, send_c, send_v, got_c, got_v,
     low_s, w_s, p_s, high_t, sent_c, sent_v, came_c, came_v,
 ):
     devices = rows * cols
     tiles = cell_ref.shape[0]
-    row, col = lax.axis_index(ROW), lax.axis_index(COL)
+    me = lax.axis_index(ROW) * cols + lax.axis_index(COL)
     barrier = pltpu.get_barrier_semaphore()
 
-    def greet(k, _):
-        pr, pc = partner(row, col, rows, cols, k)
-        pl.semaphore_signal(barrier, inc=1, device_id=(pr, pc), device_id_type=MESH)
-        return 0
-
-    lax.fori_loop(1, devices, greet, 0)
+    def greet(k):
+        pl.semaphore_signal(
+            barrier, inc=1, device_id=partner(me, devices, k), device_id_type=LOGICAL
+        )
+
+    each_partner(devices, greet)
+    for copy in loads:
+        copy.wait()
 
     counts = count_ref[...].T
     slot = lax.broadcasted_iota(jnp.int32, (devices, TILE), 1)
@@ -69,31 +76,28 @@
         stage_w[pl.ds(t * PITCH, devices), :] = jnp.where(live, wide, 0.0)
         stage_p[pl.ds(t * PITCH, devices), :] = jnp.where(live, product, 0.0)
 
-    def gather(k, _):
-        pr, pc = partner(row, col, rows, cols, k)
-        q = pr * cols + pc
-        rows_at = pl.ds(q, tiles, stride=PITCH)
-        send_c[k] = stage_c[rows_at, :].astype(jnp.int16)
-        send_v[k, 0:16, :] = stage_w[rows_at, :].astype(BF)
-        send_v[k, 16:32, :] = stage_p[rows_at, :].astype(BF)
+    def gather(g, _):
+        for j in range(8):
+            k = g * 8 + j
+            rows_at = pl.ds(partner(me, devices, k), tiles, stride=PITCH)
+            send_c[k] = stage_c[rows_at, :].astype(jnp.int16)
+            send_v[k, 0:16, :] = stage_w[rows_at, :].astype(BF)
+            send_v[k, 16:32, :] = stage_p[rows_at, :].astype(BF)
         return 0
 
-    lax.fori_loop(0, devices, gather, 0)
+    lax.fori_loop(0, devices // 8, gather, 0)
     pl.semaphore_wait(barrier, devices - 1)
 
-    def send(k, _):
-        pr, pc = partner(row, col, rows, cols, k)
+    def send(k):
+        to = partner(me, devices, k)
         pltpu.make_async_remote_copy(
-            send_c.at[k], got_c.at[k], sent_c, came_c.at[k // 8],
-            device_id=(pr, pc), device_id_type=MESH,
+            send_c.at[k], got_c.at[k], sent_c, came_c.at[k // 8], device_id=to, device_id_type=LOGICAL
         ).start()
         pltpu.make_async_remote_copy(
-            send_v.at[k], got_v.at[k], sent_v, came_v.at[k // 8],
-            device_id=(pr, pc), device_id_type=MESH,
+            send_v.at[k], got_v.at[k], sent_v, came_v.at[k // 8], device_id=to, device_id_type=LOGICAL
         ).start()
-        return 0
-
-    lax.fori_loop(1, devices, send, 0)
+
+    each_partner(devices, send)
     got_c[0] = send_c[0]
     got_v[0] = send_v[0]
     wf_ref[...] = jnp.zeros_like(wf_ref)
@@ -219,7 +223,7 @@
 
 
 def smooth(
-    rows, cols, kappa_ref, wf_ref, resp_ref, x_ref, r_ref, growth_ref,
+    rows, cols, while_waiting, kappa_ref, wf_ref, resp_ref, x_ref, r_ref, growth_ref,
     v0, v1, v2, v3, u, w, c, send_rows, send_cols, got_rows, got_cols, got_corners,
     part, parts, sent_edge, came_edge, sent_part, came_part,
 ):
@@ -362,14 +366,14 @@
     part[...] = mine
     parts[me] = mine
 
-    def tell(k, _):
-        pr, pc = partner(row, col, rows, cols, k)
+    def tell(k):
+        to = partner(me, devices, k)
         pltpu.make_async_remote_copy(
-            part, parts.at[me], sent_part, came_part, device_id=(pr, pc), device_id_type=MESH
+            part, parts.at[me], sent_part, came_part, device_id=to, device_id_type=LOGICAL
         ).start()
-        return 0
-
-    lax.fori_loop(1, devices, tell, 0)
+
+    each_partner(devices, tell)
+    while_waiting()
     others = pl.ds(1, devices - 1)
     pltpu.make_async_copy(parts.at[others], parts.at[others], came_part).wait()
     total = jnp.sum(parts[...], axis=0)
@@ -393,36 +397,62 @@
     pltpu.make_async_copy(parts.at[others], parts.at[others], sent_part).wait()
 
 
-def whole(rows, cols, cell, value, weight, count, kappa, x, r, growth, wf_out, resp_out, wf, resp, *rest):
-    first, second, keep = rest[:15], rest[15:-1], rest[-1]
-    exchange_and_bin(rows, cols, cell, value, weight, count, wf, resp, *first)
-    kept = [
-        pltpu.make_async_copy(wf, wf_out, keep.at[0]),
-        pltpu.make_async_copy(resp, resp_out, keep.at[1]),
-    ]
-    for copy in kept:
+def whole(rows, cols, *refs):
+    inputs, (x, r, growth, *kept), inside, (wf, resp) = refs[:5], refs[5:10], refs[10:15], refs[15:17]
+    first, second, moved = refs[17:32], refs[32:-1], refs[-1]
+    loads = [pltpu.make_async_copy(a, b, moved.at[i]) for i, (a, b) in enumerate(zip(inputs, inside))]
+    for copy in loads:
         copy.start()
-    smooth(rows, cols, kappa, wf, resp, x, r, growth, *second)
-    for copy in kept:
+    stores = [pltpu.make_async_copy(a, b, moved.at[5 + i]) for i, (a, b) in enumerate(zip((wf, resp), kept))]
+    exchange_and_bin(rows, cols, loads[:4], *inside[:4], wf, resp, *first)
+    loads[4].wait()
+
+    def while_waiting():
+        for copy in stores:
+            copy.start()
+
+    smooth(rows, cols, while_waiting, inside[4], wf, resp, x, r, growth, *second)
+    for copy in stores:
         copy.wait()
+
+
+def hand_over(*refs):
+    copies = [pltpu.make_async_copy(refs[i], refs[2 + i], refs[4].at[i]) for i in range(2)]
+    for copy in copies:
+        copy.start()
+    for copy in copies:
+        copy.wait()
+
+
+def deliver(x, r):
+    return pl.pallas_call(
+        hand_over,
+        out_shape=[jax.ShapeDtypeStruct(a.shape, a.dtype) for a in (x, r)],
+        in_specs=[pl.BlockSpec(memory_space=pl.ANY)] * 2,
+        out_specs=[pl.BlockSpec(memory_space=pltpu.HBM)] * 2,
+        scratch_shapes=[pltpu.SemaphoreType.DMA((2,))],
+        name="deliver",
+    )(x, r)
 
 
 def run(rows, cols, obs_cell, obs_value, obs_weight, obs_count, kappa_field):
     devices = rows * cols
     tiles = obs_cell.shape[0]
     high, wide = kappa_field.shape
+    arguments = (obs_cell, obs_value, obs_weight, obs_count, kappa_field)
     vmem = pl.BlockSpec(memory_space=pltpu.VMEM)
-    anywhere = pl.BlockSpec(memory_space=pl.ANY)
+    hbm = pl.BlockSpec(memory_space=pltpu.HBM)
     stage = (tiles * PITCH, TILE)
     work = pltpu.VMEM((high + 2 * TOP, wide + WIDE), F32)
     dma = pltpu.SemaphoreType.DMA
     shape = jax.ShapeDtypeStruct((high, wide), F32)
     return pl.pallas_call(
         functools.partial(whole, rows, cols),
-        out_shape=[shape, shape, jax.ShapeDtypeStruct((1, WIDE), F32), shape, shape],
-        in_specs=[vmem] * 5,
-        out_specs=[vmem] * 3 + [anywhere] * 2,
+        out_shape=[pltpu.VMEM((high, wide), F32), pltpu.VMEM((high, wide), F32), pltpu.VMEM((1, WIDE), F32), shape, shape],
+        in_specs=[hbm] * 5,
+        out_specs=[vmem] * 3 + [hbm] * 2,
         scratch_shapes=[
+            *[pltpu.VMEM(a.shape, a.dtype) for a in arguments],
             pltpu.VMEM((high, wide), F32),
             pltpu.VMEM((high, wide), F32),
             pltpu.VMEM(stage, jnp.int32),
@@ -452,11 +482,11 @@
             dma((8,)),
             dma,
             dma,
-            dma((2,)),
+            dma((7,)),
         ],
         name="bin_and_smooth",
         compiler_params=pltpu.CompilerParams(collective_id=0, has_side_effects=True),
-    )(obs_cell, obs_value, obs_weight, obs_count, kappa_field)
+    )(*arguments)
 
 
 def extended(x, sides, width):
@@ -531,7 +561,7 @@
     )
     return lax.cond(
         growth[0, 0] <= GROWTH_MAX,
-        lambda x, r, *rest: (x, r),
+        lambda x, r, *rest: tuple(deliver(x, r)),
         lambda x, r, *rest: step_by_step(*rest),
         x, r, weight_field, response, kappa_field,
     )

time: 85.3 us -> 75.5 us (0.89)
  Pallas kernels: 79.9 us -> 73.6 us
  local copies, waits for them, and re-layouts: 3.99 us -> 0.01 us
    pallas_call x1 -> x2, Pallas kernels: 79.9 us -> 73.6 us  [the longest x1 72.3 us: run(): pl.pallas_call(functools.partial(whole, rows, cols), out_shape=[pltpu.VME...]
    unnamed x8 -> x2, local copies, waits for them, and re-layouts: 3.99 us -> 0.01 us
where the time goes in v3:
time: 75.5 us; the launch traced here: 74.7 us
  Pallas kernels  73.6 us (97%)
  between operations  0.87 us (1%)
    pallas_call x1, Pallas kernels, run(): pl.pallas_call(functools.partial(whole, rows, cols), out_shape=[pltpu.VME...  72.3 us

profile of v3, /device:TPU:0, one launch (start us, length us, event | category | flops | bytes accessed | tf_op | source)
XLA Modules:
  0.0 74.7 jit_solution(11236558810924973740)
XLA Ops:
  0.6 0.0 copy-start
  0.6 72.3 %bin_and_smooth.1 = (f32[512,512]{1,0:T(8,128)S(1)}, f32[512,512]{1,0:T(8,128)S(1)}, f32[1,128]{1,0:T(1,128)S(1)}, f32[512,512]{1,0:T(8,128)}, f32[512,512]{1,0:T(8,128)}) custom-call(s32[16,128,128]{2,1,0:T(8,128)} %bitcast.7, bf16[16,128,128]{2,1,0:T(8,128)(2,1)} %bitcast.8, bf16[16,128,128]{2,1,0:T(8,128)(2,1)} %bitcast.9, s32[16,128]{1,0:T(8,128)} %bitcast.10, ...), custom_call_target="tpu_custom_call" | custom-call | tf_op jit(solution)/shard_map/bin_and_smooth/pallas_call | solution.py:449
  73.0 0.0 copy-done
  73.0 1.6 %conditional.1 = ((f32[512,512]{1,0:T(8,128)}, f32[512,512]{1,0:T(8,128)})) conditional(s32[]{:T(128)} %bitcast.4, (f32[512,512]{1,0:T(8,128)}, f32[512,512]{1,0:T(8,128)}, f32[512,512]{1,0:T(8,128)S(1)}) %tuple.43, (f32[512,512]{1,0:T(8,128)S(1)}, f32[512,512]{1,0:T(8,128)S(1)}) %tuple.15), branch_computations={%region_0.19_spmd, %region_19.20_spmd} | conditional | flops 42467336 | bytes 58017148 | solution.py:562
  73.2 1.3 %deliver.1 = (f32[512,512]{1,0:T(8,128)}, f32[512,512]{1,0:T(8,128)}) custom-call(f32[512,512]{1,0:T(8,128)S(1)} %get-tuple-element.13.refs_0_, f32[512,512]{1,0:T(8,128)S(1)} %get-tuple-element.14.refs_1_), custom_call_target="tpu_custom_call" | custom-call | tf_op jit(solution)/shard_map/cond/branch_1_fun/deliver/pallas_call | solution.py:428
Async XLA Ops:
  0.6 72.3 %copy-start = (f32[512,512]{1,0:T(8,128)S(1)}, f32[512,512]{1,0:T(8,128)}, u32[]{:S(2)}) copy-start(f32[512,512]{1,0:T(8,128)} %refs_4_.1) | copy-start | bytes 3145732

commit v4 on v3

--- a/solution.py
+++ b/solution.py
@@ -17,6 +17,7 @@
 F32 = jnp.float32
 PITCH = 136
 STRIDE = 5
+GROUP = 16
 
 smooth_weight = 0.05
 
@@ -24,7 +25,7 @@
 SHIFT = 5.0
 GROWTH_MAX = 1000.0
 EDGE = 8
-TOP = 16
+RIM = 6
 WIDE = 128
 
 
@@ -45,9 +46,9 @@
 
 
 def exchange_and_bin(
-    rows, cols, loads, cell_ref, value_ref, weight_ref, count_ref, wf_ref, resp_ref,
+    rows, cols, loads, ready, sent_out, cell_ref, value_ref, weight_ref, count_ref, wf_ref, resp_ref,
     stage_c, stage_w, stage_p, send_c, send_v, got_c, got_v,
-    low_s, w_s, p_s, high_t, sent_c, sent_v, came_c, came_v,
+    low_s, w_s, p_s, high_s, sent_c, sent_v, came_c, came_v,
 ):
     devices = rows * cols
     tiles = cell_ref.shape[0]
@@ -86,18 +87,20 @@
         return 0
 
     lax.fori_loop(0, devices // 8, gather, 0)
+    ready()
     pl.semaphore_wait(barrier, devices - 1)
 
     def send(k):
         to = partner(me, devices, k)
         pltpu.make_async_remote_copy(
-            send_c.at[k], got_c.at[k], sent_c, came_c.at[k // 8], device_id=to, device_id_type=LOGICAL
+            send_c.at[k], got_c.at[k], sent_c, came_c.at[k // GROUP], device_id=to, device_id_type=LOGICAL
         ).start()
         pltpu.make_async_remote_copy(
-            send_v.at[k], got_v.at[k], sent_v, came_v.at[k // 8], device_id=to, device_id_type=LOGICAL
+            send_v.at[k], got_v.at[k], sent_v, came_v.at[k // GROUP], device_id=to, device_id_type=LOGICAL
         ).start()
 
     each_partner(devices, send)
+    sent_out()
     got_c[0] = send_c[0]
     got_v[0] = send_v[0]
     wf_ref[...] = jnp.zeros_like(wf_ref)
@@ -111,21 +114,21 @@
     across = wf_ref.shape[1] // TILE
 
     def bin_group(g):
-        code = got_c[pl.ds(g * 8, 8)].reshape(128, 128).astype(jnp.int32)
+        code = got_c[pl.ds(g * GROUP, GROUP)].reshape(GROUP * tiles, 128).astype(jnp.int32)
         low_s[...] = jnp.bitwise_and(code, 63).astype(F32)
-        high_t[...] = jnp.right_shift(code, 6).astype(F32).T
-        for s in range(8):
-            w_s[pl.ds(s * 16, 16), :] = got_v[g * 8 + s, 0:16, :].astype(F32)
-            p_s[pl.ds(s * 16, 16), :] = got_v[g * 8 + s, 16:32, :].astype(F32)
+        high_s[...] = jnp.right_shift(code, 6).astype(F32)
+        for s in range(GROUP):
+            w_s[pl.ds(s * 16, 16), :] = got_v[g * GROUP + s, 0:16, :].astype(F32)
+            p_s[pl.ds(s * 16, 16), :] = got_v[g * GROUP + s, 16:32, :].astype(F32)
         for t in range(tiles):
             total = None
-            for pair in range(4):
+            for pair in range(GROUP // 2):
                 left, right = [], []
                 for s in (2 * pair, 2 * pair + 1):
                     r = s * 16 + t
-                    low, w, p = (
+                    low, high, w, p = (
                         jnp.broadcast_to(ref[pl.ds(r, 1), :], (16, 128)).astype(BF)
-                        for ref in (low_s, w_s, p_s)
+                        for ref in (low_s, high_s, w_s, p_s)
                     )
                     hits = [low == ids for ids in low_ids]
                     left.append(
@@ -135,9 +138,9 @@
                             axis=0,
                         )
                     )
-                    high = jnp.broadcast_to(high_t[:, r : r + 1], (128, 128)).astype(BF)
+                    turned = jnp.concatenate([high] * 8, axis=0).T
                     for v in range(8):
-                        part = high[16 * v : 16 * v + 16]
+                        part = turned[16 * v : 16 * v + 16]
                         right.append(
                             jnp.concatenate([jnp.where(part == ids, one, zero) for ids in high_ids], axis=1)
                         )
@@ -163,16 +166,16 @@
     def step(g, _):
         @pl.when(g == 0)
         def _():
-            arrived(1, 7, 0)
+            arrived(1, GROUP - 1, 0)
 
         @pl.when(g > 0)
         def _():
-            arrived(g * 8, 8, g)
+            arrived(g * GROUP, GROUP, g)
 
         bin_group(g)
         return 0
 
-    lax.fori_loop(0, devices // 8, step, 0)
+    lax.fori_loop(0, devices // GROUP, step, 0)
     out = pl.ds(1, devices - 1)
     pltpu.make_async_copy(send_c.at[out], send_c.at[out], sent_c).wait()
     pltpu.make_async_copy(send_v.at[out], send_v.at[out], sent_v).wait()
@@ -222,142 +225,210 @@
     return x, r, growth
 
 
-def smooth(
-    rows, cols, while_waiting, kappa_ref, wf_ref, resp_ref, x_ref, r_ref, growth_ref,
-    v0, v1, v2, v3, u, w, c, send_rows, send_cols, got_rows, got_cols, got_corners,
-    part, parts, sent_edge, came_edge, sent_part, came_part,
-):
-    devices = rows * cols
-    high, wide = kappa_ref.shape
-    row, col = lax.axis_index(ROW), lax.axis_index(COL)
-    me = row * cols + col
-    above, below = (row + rows - 1) % rows, (row + 1) % rows
-    before, after = (col + cols - 1) % cols, (col + 1) % cols
-    has_above = jnp.where(row > 0, 1.0, 0.0).astype(F32)
-    has_below = jnp.where(row < rows - 1, 1.0, 0.0).astype(F32)
-    has_before = jnp.where(col > 0, 1.0, 0.0).astype(F32)
-    has_after = jnp.where(col < cols - 1, 1.0, 0.0).astype(F32)
-    tall = high + 2 * TOP
-    full = wide + WIDE
-    own_rows, own_cols = pl.ds(TOP, high), pl.ds(0, wide)
-
-    fields = (v0, w, c)
-    for ref in (v0, w, c, u, v1, v2):
-        ref[pl.ds(0, TOP), :] = jnp.zeros((TOP, full), F32)
-        ref[pl.ds(TOP + high, TOP), :] = jnp.zeros((TOP, full), F32)
-    v0[own_rows, own_cols] = resp_ref[...]
-    w[own_rows, own_cols] = (wf_ref[...] - SHIFT) * SCALE
-    c[own_rows, own_cols] = kappa_ref[...] + 4.0
-    lane = lax.broadcasted_iota(jnp.int32, (WIDE, WIDE), 1)
-    for f, ref in enumerate(fields):
-        send_rows[0, f] = ref[pl.ds(TOP, EDGE), own_cols]
-        send_rows[1, f] = ref[pl.ds(TOP + high - EDGE, EDGE), own_cols]
-        for i in range(high // WIDE):
-            block = pl.ds(TOP + i * WIDE, WIDE)
-            left = ref[block, pl.ds(0, WIDE)]
-            right = ref[block, pl.ds(wide - WIDE, WIDE)]
-            turned = jnp.where(lane < 64, left, right).T
-            send_cols[0, f, :, pl.ds(i * WIDE, WIDE)] = turned[0:EDGE]
-            send_cols[1, f, :, pl.ds(i * WIDE, WIDE)] = turned[WIDE - EDGE :]
-
-    def copies():
-        first, last = pl.ds(0, WIDE), pl.ds(high - WIDE, WIDE)
+class Edges:
+    def __init__(self, rows, cols, rows_out, cols_out, rows_in, cols_in, corners, sent, came):
+        row, col = lax.axis_index(ROW), lax.axis_index(COL)
+        above, below = lax.rem(row + rows - 1, rows), lax.rem(row + 1, rows)
+        before, after = lax.rem(col + cols - 1, cols), lax.rem(col + 1, cols)
+        self.rows_out, self.cols_out = rows_out, cols_out
+        self.rows_in, self.cols_in, self.corners = rows_in, cols_in, corners
+        last = cols_out.shape[2] - 1
         plan = [
-            (send_rows.at[0], got_rows.at[1], above, col),
-            (send_rows.at[1], got_rows.at[0], below, col),
-            (send_cols.at[0], got_cols.at[1], row, before),
-            (send_cols.at[1], got_cols.at[0], row, after),
-            (send_cols.at[0, :, :, first], got_corners.at[3], above, before),
-            (send_cols.at[0, :, :, last], got_corners.at[1], below, before),
-            (send_cols.at[1, :, :, first], got_corners.at[2], above, after),
-            (send_cols.at[1, :, :, last], got_corners.at[0], below, after),
+            (rows_out.at[0], rows_in.at[1], above, col),
+            (rows_out.at[1], rows_in.at[0], below, col),
+            (cols_out.at[0], cols_in.at[1], row, before),
+            (cols_out.at[1], cols_in.at[0], row, after),
+            (cols_out.at[0, :, 0], corners.at[3], above, before),
+            (cols_out.at[0, :, last], corners.at[1], below, before),
+            (cols_out.at[1, :, 0], corners.at[2], above, after),
+            (cols_out.at[1, :, last], corners.at[0], below, after),
         ]
-        return [
+        self.copies = [
             pltpu.make_async_remote_copy(
-                source, target, sent_edge.at[i], came_edge.at[i], device_id=(pr, pc), device_id_type=MESH
+                source, target, sent.at[i], came.at[i], device_id=(pr, pc), device_id_type=MESH
             )
             for i, (source, target, pr, pc) in enumerate(plan)
         ]
 
-    edges = copies()
-    for copy in edges:
-        copy.start()
-    for copy in edges:
-        copy.wait()
-    gap = jnp.zeros((WIDE - 2 * EDGE, WIDE), F32)
-    for f, ref in enumerate(fields):
-        keep = (has_above, has_below, has_before, has_after) if f == 0 else (1.0, 1.0, 1.0, 1.0)
-        ref[pl.ds(TOP - EDGE, EDGE), own_cols] = got_rows[0, f] * keep[0]
-        ref[pl.ds(TOP + high, EDGE), own_cols] = got_rows[1, f] * keep[1]
-
-        def turned(left, right):
-            return jnp.concatenate([right * keep[3], gap, left * keep[2]], axis=0).T
-
-        beside = pl.ds(wide, WIDE)
-        for i in range(high // WIDE):
-            at = pl.ds(i * WIDE, WIDE)
-            ref[pl.ds(TOP + i * WIDE, WIDE), beside] = turned(got_cols[0, f, :, at], got_cols[1, f, :, at])
-        upper = turned(got_corners[0, f], got_corners[1, f])
-        ref[pl.ds(TOP - EDGE, EDGE), beside] = upper[WIDE - EDGE :] * keep[0]
-        lower = turned(got_corners[2, f], got_corners[3, f])
-        ref[pl.ds(TOP + high, EDGE), beside] = lower[0:EDGE] * keep[1]
-
-    lanes = lax.broadcasted_iota(jnp.int32, (1, full), 1)
-    side = jnp.where(lanes < wide, 1.0, jnp.where(lanes < wide + 64, has_after, has_before)).astype(F32)
-
-    def laplace(ref, at, size, center):
-        tall_block = jnp.concatenate(
-            [ref[pl.ds(at - 8, 8), :], center, ref[pl.ds(at + size, 8), :]], axis=0
-        )
-        up = pltpu.roll(tall_block, 1, 0)[8 : 8 + size]
-        down = pltpu.roll(tall_block, size + 15, 0)[8 : 8 + size]
-        sideways = pltpu.roll(center, 1, 1) + pltpu.roll(center, full - 1, 1)
-        return c[pl.ds(at, size), :] * center - (up + down + sideways)
-
-    def inner(ref, at, size, mask):
-        u[pl.ds(at, size), :] = laplace(ref, at, size, ref[pl.ds(at, size), :]) * mask
-
-    def outer(ref, out, at, size, mask):
-        here = pl.ds(at, size)
-        result = w[here, :] * ref[here, :] + (smooth_weight * SCALE) * laplace(u, at, size, u[here, :])
-        out[here, :] = result * mask
-        return result
-
-    def fold(x):
-        total = x[:, 0:WIDE]
-        for i in range(1, wide // WIDE):
-            total = total + x[:, i * WIDE : (i + 1) * WIDE]
-        return total.reshape(-1, 8, WIDE).sum(axis=0)
-
-    size = 32
+    def start(self):
+        for copy in self.copies:
+            copy.start()
+
+    def wait(self):
+        for copy in self.copies:
+            copy.wait()
+
+
+def lay_out(ref, field):
+    high, wide = field.shape
+    strip = high // 8
+    for s in range(8):
+        for j in range(wide // WIDE):
+            ref[j, pl.ds(RIM * 8 + s, strip, stride=8), :] = field[s * strip : (s + 1) * strip, j * WIDE : (j + 1) * WIDE]
+
+
+def group(i, n=1):
+    return pl.ds(i * 8, n * 8)
+
+
+def pack_edges(ref, f, edges, top, bottom):
+    lane = lax.broadcasted_iota(jnp.int32, (8, WIDE), 1)
+    tiles = ref.shape[0] - 1
+    edges.rows_out[0, f] = top
+    edges.rows_out[1, f] = bottom
+    for q in range(edges.cols_out.shape[2]):
+        left, right = jnp.zeros((8, WIDE), F32), jnp.zeros((8, WIDE), F32)
+        for n in range(16):
+            slot = (lane >= 8 * n) & (lane < 8 * n + 8)
+            at = group(RIM + 16 * q + n)
+            left = jnp.where(slot, pltpu.roll(ref[0, at, :], 8 * n, 1), left)
+            right = jnp.where(slot, pltpu.roll(ref[tiles - 1, at, :], (8 * n + 8) % WIDE, 1), right)
+        edges.cols_out[0, f, q] = left
+        edges.cols_out[1, f, q] = right
+
+
+def fill_edges(ref, f, edges, keep):
+    lane = lax.broadcasted_iota(jnp.int32, (8, WIDE), 1)
+    sub = lax.broadcasted_iota(jnp.int32, (8, WIDE), 0)
+    tiles = ref.shape[0] - 1
+    strip = ref.shape[1] // 8 - 2 * RIM
+    above, below, before, after = keep
+
+    def beside(left, right, n):
+        left = pltpu.roll(left, (120 - 8 * n) % WIDE, 1)
+        right = pltpu.roll(right, (WIDE - 8 * n) % WIDE, 1)
+        return jnp.where(lane < 8, right * after, jnp.where(lane >= 120, left * before, 0.0))
+
+    for i in range(strip):
+        q, n = i // 16, i % 16
+        ref[tiles, group(RIM + i), :] = beside(edges.cols_in[0, f, q], edges.cols_in[1, f, q], n)
+    for j in range(tiles + 1):
+        for i in range(RIM):
+            if j < tiles:
+                up = edges.rows_in[0, f, EDGE - RIM + i : EDGE - RIM + i + 1, j * WIDE : (j + 1) * WIDE]
+                down = edges.rows_in[1, f, i : i + 1, j * WIDE : (j + 1) * WIDE]
+                up, down = (jnp.broadcast_to(x, (8, WIDE)) for x in (up, down))
+            else:
+                up = beside(edges.corners[0, f], edges.corners[1, f], 16 - RIM + i)
+                down = beside(edges.corners[2, f], edges.corners[3, f], i)
+                up, down = pltpu.roll(up, 1, 0), pltpu.roll(down, 7, 0)
+            inside = pltpu.roll(ref[j, group(strip + i), :], 1, 0)
+            ref[j, group(i), :] = jnp.where(sub == 0, up * above, inside)
+            inside = pltpu.roll(ref[j, group(RIM + i), :], 7, 0)
+            ref[j, group(RIM + strip + i), :] = jnp.where(sub == 7, down * below, inside)
+
+
+def smooth(
+    rows, cols, while_waiting, early, late, wf_ref, resp_ref, x_ref, r_ref, growth_ref,
+    v0, v1, v2, v3, u, w, c, y1, y2, y3, part, parts, sent_part, came_part,
+):
+    devices = rows * cols
+    high, wide = x_ref.shape
+    tiles, strip = wide // WIDE, high // 8
+    row, col = lax.axis_index(ROW), lax.axis_index(COL)
+    me = row * cols + col
+    keep = tuple(
+        jnp.where(there, 1.0, 0.0).astype(F32)
+        for there in (row > 0, row < rows - 1, col > 0, col < cols - 1)
+    )
+
+    lay_out(v0, resp_ref[...])
+    lay_out(w, (wf_ref[...] - SHIFT) * SCALE)
+    first, last = slice(0, EDGE), slice(high - EDGE, high)
+    pack_edges(v0, 0, late, resp_ref[first, :], resp_ref[last, :])
+    pack_edges(w, 1, late, (wf_ref[first, :] - SHIFT) * SCALE, (wf_ref[last, :] - SHIFT) * SCALE)
+    late.start()
+    early.wait()
+    fill_edges(c, 0, early, (1.0,) * 4)
+    late.wait()
+    fill_edges(v0, 0, late, keep)
+    fill_edges(w, 1, late, (1.0,) * 4)
+
+    lane = lax.broadcasted_iota(jnp.int32, (8, WIDE), 1)
+    sub = lax.broadcasted_iota(jnp.int32, (8, WIDE), 0)
+    side = jnp.where(lane < 64, keep[3], keep[2])
+    upper = jnp.where(sub == 0, keep[0], 1.0)
+    lower = jnp.where(sub == 7, keep[1], 1.0)
+
+    def laplace(ref, i, n):
+        size = n * 8
+        lanes = lax.broadcasted_iota(jnp.int32, (size, WIDE), 1)
+        tall = [ref[j, group(i - 1, n + 2), :] for j in range(tiles + 1)]
+        here = [x[8 : 8 + size] for x in tall]
+        later = [pltpu.roll(x, 1, 1) for x in here]
+        sooner = [pltpu.roll(x, WIDE - 1, 1) for x in here]
+        out = []
+        for j in range(tiles + 1):
+            left = jnp.where(lanes == 0, later[j - 1], later[j])
+            right = jnp.where(lanes == WIDE - 1, sooner[(j + 1) % (tiles + 1)], sooner[j])
+            beside = (tall[j][0:size] + tall[j][16 : 16 + size]) + (left + right)
+            out.append(c[j, group(i, n), :] * here[j] - beside)
+        return out, here
+
+    def masked(x, n, j, edge):
+        if edge is not None:
+            x = x * jnp.concatenate([edge] * n, axis=0)
+        if j == tiles:
+            x = x * jnp.concatenate([side] * n, axis=0)
+        return x
+
+    def inner(ref, i, n, edge=None):
+        news, olds = laplace(ref, i, n)
+        news = [masked(x, n, j, edge) for j, x in enumerate(news)]
+        for j, x in enumerate(news):
+            u[j, group(i, n), :] = x
+        return news[:tiles], olds[:tiles]
+
+    def outer(ref, out, i, n, edge=None):
+        news, olds = [], []
+        for j, x in enumerate(laplace(u, i, n)[0]):
+            old = ref[j, group(i, n), :]
+            new = masked(w[j, group(i, n), :] * old + (smooth_weight * SCALE) * x, n, j, edge)
+            out[j, group(i, n), :] = new
+            news.append(new)
+            olds.append(old)
+        return news[:tiles], olds[:tiles]
+
+    def fold(pairs, n):
+        total = None
+        for a, b in pairs:
+            product = a * b
+            for i in range(n):
+                piece = product[i * 8 : i * 8 + 8]
+                total = piece if total is None else total + piece
+        return total
+
+    n = 16
     zero = jnp.zeros((8, WIDE), F32)
     moments = []
     for step, (ref, out) in enumerate(((v0, v1), (v1, v2), (v2, v3))):
-        inner(ref, TOP - EDGE, EDGE, side * has_above)
-        inner(ref, TOP + high, EDGE, side * has_below)
-
-        def rows_of_u(i, _, ref=ref):
-            inner(ref, pl.multiple_of(TOP + i * size, 8), size, side)
-            return 0
-
-        lax.fori_loop(0, high // size, rows_of_u, 0)
-        if step < 2:
-            outer(ref, out, TOP - EDGE, EDGE, side * has_above)
-            outer(ref, out, TOP + high, EDGE, side * has_below)
-
-        def rows_of_v(i, sums, ref=ref, out=out, step=step):
-            at = pl.multiple_of(TOP + i * size, 8)
-            new = outer(ref, out, at, size, side)[:, 0:wide]
-            old = ref[pl.ds(at, size), own_cols]
-            terms = [old * new]
+        rim = RIM - 1 - 2 * step
+        inner(ref, RIM - rim, rim, upper)
+        inner(ref, RIM + strip, rim, lower)
+
+        def rows_of_u(k, sums, ref=ref, step=step):
+            news, olds = inner(ref, RIM + k * n, n)
+            if step < 2:
+                return sums
+            weighted = [w[j, group(RIM + k * n, n), :] * x for j, x in enumerate(olds)]
+            return sums[0] + fold(zip(weighted, olds), n), sums[1] + fold(zip(news, news), n)
+
+        sums = lax.fori_loop(0, strip // n, rows_of_u, (zero,) * (0, 0, 2)[step])
+        if step == 2:
+            moments.append(sums[0] + (smooth_weight * SCALE) * sums[1])
+            break
+        outer(ref, out, RIM - rim + 1, rim - 1, upper)
+        outer(ref, out, RIM + strip, rim - 1, lower)
+
+        def rows_of_v(k, sums, ref=ref, out=out, step=step):
+            news, olds = outer(ref, out, RIM + k * n, n)
+            terms = [fold(zip(olds, news), n), fold(zip(news, news), n)]
             if step == 0:
-                terms.append(old * old)
-            if step < 2:
-                terms.append(new * new)
-            return tuple(s + fold(t) for s, t in zip(sums, terms))
-
-        sums = lax.fori_loop(0, high // size, rows_of_v, (zero,) * (3, 2, 1)[step])
-        moments += [sums[1], sums[0], sums[2]] if step == 0 else list(sums)
+                terms.append(fold(zip(olds, olds), n))
+            return tuple(s + t for s, t in zip(sums, terms))
+
+        sums = lax.fori_loop(0, strip // n, rows_of_v, (zero,) * (3, 2)[step])
+        moments += [sums[2], sums[0], sums[1]] if step == 0 else list(sums)
 
     column = lax.broadcasted_iota(jnp.int32, (1, WIDE), 1)
     mine = jnp.zeros((1, WIDE), F32)
@@ -374,6 +445,21 @@
 
     each_partner(devices, tell)
     while_waiting()
+
+    def rows_of_last(k, _):
+        outer(v2, v3, RIM + k * n, n)
+        return 0
+
+    lax.fori_loop(0, strip // n, rows_of_last, 0)
+
+    def straighten(s, _):
+        for j in range(tiles):
+            place = (pl.ds(s * strip, strip), pl.ds(j * WIDE, WIDE))
+            for ref, flat in ((v1, y1), (v2, y2), (v3, y3)):
+                flat[place] = ref[j, pl.ds(RIM * 8 + s, strip, stride=8), :]
+        return 0
+
+    lax.fori_loop(0, 8, straighten, 0)
     others = pl.ds(1, devices - 1)
     pltpu.make_async_copy(parts.at[others], parts.at[others], came_part).wait()
     total = jnp.sum(parts[...], axis=0)
@@ -381,37 +467,43 @@
     xs, rs, growth = solve([jnp.broadcast_to(value, (1, WIDE)) for value in m])
     growth_ref[...] = growth
 
-    def combine(i, _):
-        at = pl.ds(pl.multiple_of(i * size, 8), size)
-        held = pl.ds(pl.multiple_of(TOP + i * size, 8), size)
-
-        def spread(value):
-            return jnp.concatenate([jnp.broadcast_to(value, (size, WIDE))] * (wide // WIDE), axis=1)
-
-        basis = [ref[held, own_cols] for ref in (v0, v1, v2, v3)]
-        x_ref[at, :] = sum(spread(k * SCALE) * v for k, v in zip(xs, basis))
-        r_ref[at, :] = sum(spread(k) * v for k, v in zip(rs, basis))
+    def spread(value):
+        return jnp.concatenate([jnp.broadcast_to(value, (32, WIDE))] * tiles, axis=1)
+
+    def combine(k, _):
+        at = pl.ds(k * 32, 32)
+        basis = [ref[at, :] for ref in (resp_ref, y1, y2, y3)]
+        x_ref[at, :] = sum(spread(a * SCALE) * v for a, v in zip(xs, basis))
+        r_ref[at, :] = sum(spread(a) * v for a, v in zip(rs, basis))
         return 0
 
-    lax.fori_loop(0, high // size, combine, 0)
+    lax.fori_loop(0, high // 32, combine, 0)
     pltpu.make_async_copy(parts.at[others], parts.at[others], sent_part).wait()
 
 
 def whole(rows, cols, *refs):
     inputs, (x, r, growth, *kept), inside, (wf, resp) = refs[:5], refs[5:10], refs[10:15], refs[15:17]
-    first, second, moved = refs[17:32], refs[32:-1], refs[-1]
+    first, second, moved = refs[17:32], refs[32:46], refs[60]
+    early, late = Edges(rows, cols, *refs[46:53]), Edges(rows, cols, *refs[53:60])
+    kappa, c = inside[4], second[6]
     loads = [pltpu.make_async_copy(a, b, moved.at[i]) for i, (a, b) in enumerate(zip(inputs, inside))]
     for copy in loads:
         copy.start()
     stores = [pltpu.make_async_copy(a, b, moved.at[5 + i]) for i, (a, b) in enumerate(zip((wf, resp), kept))]
-    exchange_and_bin(rows, cols, loads[:4], *inside[:4], wf, resp, *first)
-    loads[4].wait()
+
+    def ready():
+        loads[4].wait()
+        lay_out(c, kappa[...] + 4.0)
+        high = kappa.shape[0]
+        pack_edges(c, 0, early, kappa[0:EDGE, :] + 4.0, kappa[high - EDGE : high, :] + 4.0)
+
+    exchange_and_bin(rows, cols, loads[:4], ready, early.start, *inside[:4], wf, resp, *first)
 
     def while_waiting():
         for copy in stores:
             copy.start()
 
-    smooth(rows, cols, while_waiting, inside[4], wf, resp, x, r, growth, *second)
+    smooth(rows, cols, while_waiting, early, late, wf, resp, x, r, growth, *second)
     for copy in stores:
         copy.wait()
 
@@ -443,7 +535,13 @@
     vmem = pl.BlockSpec(memory_space=pltpu.VMEM)
     hbm = pl.BlockSpec(memory_space=pltpu.HBM)
     stage = (tiles * PITCH, TILE)
-    work = pltpu.VMEM((high + 2 * TOP, wide + WIDE), F32)
+    work = pltpu.VMEM((wide // WIDE + 1, (high // 8 + 2 * RIM) * 8, WIDE), F32)
+
+    def edges(count):
+        ends = pltpu.VMEM((2, count, EDGE, wide), F32)
+        sides = pltpu.VMEM((2, count, high // WIDE, 8, WIDE), F32)
+        return [ends, sides, ends, sides, pltpu.VMEM((4, count, 8, WIDE), F32), dma((8,)), dma((8,))]
+
     dma = pltpu.SemaphoreType.DMA
     shape = jax.ShapeDtypeStruct((high, wide), F32)
     return pl.pallas_call(
@@ -462,26 +560,19 @@
             pltpu.VMEM((devices, 2 * tiles, TILE), BF),
             pltpu.VMEM((devices, tiles, TILE), jnp.int16),
             pltpu.VMEM((devices, 2 * tiles, TILE), BF),
-            pltpu.VMEM((128, 128), F32),
-            pltpu.VMEM((128, 128), F32),
-            pltpu.VMEM((128, 128), F32),
-            pltpu.VMEM((128, 128), F32),
+            *[pltpu.VMEM((GROUP * tiles, TILE), F32)] * 4,
             dma,
             dma,
-            dma((devices // 8,)),
-            dma((devices // 8,)),
+            dma((devices // GROUP,)),
+            dma((devices // GROUP,)),
             *[work] * 7,
-            pltpu.VMEM((2, 3, EDGE, wide), F32),
-            pltpu.VMEM((2, 3, EDGE, high), F32),
-            pltpu.VMEM((2, 3, EDGE, wide), F32),
-            pltpu.VMEM((2, 3, EDGE, high), F32),
-            pltpu.VMEM((4, 3, EDGE, WIDE), F32),
+            *[pltpu.VMEM((high, wide), F32)] * 3,
             pltpu.VMEM((1, WIDE), F32),
             pltpu.VMEM((devices, 1, WIDE), F32),
-            dma((8,)),
-            dma((8,)),
             dma,
             dma,
+            *edges(1),
+            *edges(2),
             dma((7,)),
         ],
         name="bin_and_smooth",

time: 75.5 us -> 62 us (0.82)
  Pallas kernels: 73.6 us -> 60.5 us
    pallas_call x1, Pallas kernels: 72.3 us -> 59.2 us  [run(): pl.pallas_call(functools.partial(whole, rows, cols), out_shape=[pltpu.VME...]
where the time goes in v4:
time: 62 us; the launch traced here: 61.6 us
  Pallas kernels  60.5 us (98%)
  between operations  0.87 us (1%)
    pallas_call x1, Pallas kernels, run(): pl.pallas_call(functools.partial(whole, rows, cols), out_shape=[pltpu.VME...  59.2 us
    pallas_call x1, Pallas kernels, deliver(): pl.pallas_call(hand_over, out_shape=[jax.ShapeDtypeStruct(a.shape, a.dtyp...  1.33 us

profile of v4, /device:TPU:0, one launch (start us, length us, event | category | flops | bytes accessed | tf_op | source)
XLA Modules:
  0.0 61.6 jit_solution(4044905819356114111)
XLA Ops:
  0.6 0.0 copy-start
  0.6 59.2 %bin_and_smooth.1 = (f32[512,512]{1,0:T(8,128)S(1)}, f32[512,512]{1,0:T(8,128)S(1)}, f32[1,128]{1,0:T(1,128)S(1)}, f32[512,512]{1,0:T(8,128)}, f32[512,512]{1,0:T(8,128)}) custom-call(s32[16,128,128]{2,1,0:T(8,128)} %bitcast.7, bf16[16,128,128]{2,1,0:T(8,128)(2,1)} %bitcast.8, bf16[16,128,128]{2,1,0:T(8,128)(2,1)} %bitcast.9, s32[16,128]{1,0:T(8,128)} %bitcast.10, ...), custom_call_target="tpu_custom_call" | custom-call | tf_op jit(solution)/shard_map/bin_and_smooth/pallas_call | solution.py:547
  59.9 0.0 copy-done
  59.9 1.6 %conditional.1 = ((f32[512,512]{1,0:T(8,128)}, f32[512,512]{1,0:T(8,128)})) conditional(s32[]{:T(128)} %bitcast.4, (f32[512,512]{1,0:T(8,128)}, f32[512,512]{1,0:T(8,128)}, f32[512,512]{1,0:T(8,128)S(1)}) %tuple.43, (f32[512,512]{1,0:T(8,128)S(1)}, f32[512,512]{1,0:T(8,128)S(1)}) %tuple.15), branch_computations={%region_0.19_spmd, %region_19.20_spmd} | conditional | flops 42467336 | bytes 58017148 | solution.py:653
  60.1 1.3 %deliver.1 = (f32[512,512]{1,0:T(8,128)}, f32[512,512]{1,0:T(8,128)}) custom-call(f32[512,512]{1,0:T(8,128)S(1)} %get-tuple-element.13.refs_0_, f32[512,512]{1,0:T(8,128)S(1)} %get-tuple-element.14.refs_1_), custom_call_target="tpu_custom_call" | custom-call | tf_op jit(solution)/shard_map/cond/branch_1_fun/deliver/pallas_call | solution.py:520
Async XLA Ops:
  0.6 59.2 %copy-start = (f32[512,512]{1,0:T(8,128)S(1)}, f32[512,512]{1,0:T(8,128)}, u32[]{:S(2)}) copy-start(f32[512,512]{1,0:T(8,128)} %refs_4_.1) | copy-start | bytes 3145732

commit v5 on v4

--- a/solution.py
+++ b/solution.py
@@ -319,7 +319,7 @@
 
 
 def smooth(
-    rows, cols, while_waiting, early, late, wf_ref, resp_ref, x_ref, r_ref, growth_ref,
+    rows, cols, while_waiting, early, middle, late, wf_ref, resp_ref, x_ref, r_ref, growth_ref,
     v0, v1, v2, v3, u, w, c, y1, y2, y3, part, parts, sent_part, came_part,
 ):
     devices = rows * cols
@@ -332,17 +332,17 @@
         for there in (row > 0, row < rows - 1, col > 0, col < cols - 1)
     )
 
+    first, last = slice(0, EDGE), slice(high - EDGE, high)
     lay_out(v0, resp_ref[...])
+    pack_edges(v0, 0, middle, resp_ref[first, :], resp_ref[last, :])
+    middle.start()
     lay_out(w, (wf_ref[...] - SHIFT) * SCALE)
-    first, last = slice(0, EDGE), slice(high - EDGE, high)
-    pack_edges(v0, 0, late, resp_ref[first, :], resp_ref[last, :])
-    pack_edges(w, 1, late, (wf_ref[first, :] - SHIFT) * SCALE, (wf_ref[last, :] - SHIFT) * SCALE)
+    pack_edges(w, 0, late, (wf_ref[first, :] - SHIFT) * SCALE, (wf_ref[last, :] - SHIFT) * SCALE)
     late.start()
     early.wait()
     fill_edges(c, 0, early, (1.0,) * 4)
-    late.wait()
-    fill_edges(v0, 0, late, keep)
-    fill_edges(w, 1, late, (1.0,) * 4)
+    middle.wait()
+    fill_edges(v0, 0, middle, keep)
 
     lane = lax.broadcasted_iota(jnp.int32, (8, WIDE), 1)
     sub = lax.broadcasted_iota(jnp.int32, (8, WIDE), 0)
@@ -398,7 +398,7 @@
                 total = piece if total is None else total + piece
         return total
 
-    n = 16
+    n = 32
     zero = jnp.zeros((8, WIDE), F32)
     moments = []
     for step, (ref, out) in enumerate(((v0, v1), (v1, v2), (v2, v3))):
@@ -417,6 +417,9 @@
         if step == 2:
             moments.append(sums[0] + (smooth_weight * SCALE) * sums[1])
             break
+        if step == 0:
+            late.wait()
+            fill_edges(w, 0, late, (1.0,) * 4)
         outer(ref, out, RIM - rim + 1, rim - 1, upper)
         outer(ref, out, RIM + strip, rim - 1, lower)
 
@@ -483,8 +486,8 @@
 
 def whole(rows, cols, *refs):
     inputs, (x, r, growth, *kept), inside, (wf, resp) = refs[:5], refs[5:10], refs[10:15], refs[15:17]
-    first, second, moved = refs[17:32], refs[32:46], refs[60]
-    early, late = Edges(rows, cols, *refs[46:53]), Edges(rows, cols, *refs[53:60])
+    first, second, moved = refs[17:32], refs[32:46], refs[67]
+    early, middle, late = (Edges(rows, cols, *refs[i : i + 7]) for i in (46, 53, 60))
     kappa, c = inside[4], second[6]
     loads = [pltpu.make_async_copy(a, b, moved.at[i]) for i, (a, b) in enumerate(zip(inputs, inside))]
     for copy in loads:
@@ -503,7 +506,7 @@
         for copy in stores:
             copy.start()
 
-    smooth(rows, cols, while_waiting, early, late, wf, resp, x, r, growth, *second)
+    smooth(rows, cols, while_waiting, early, middle, late, wf, resp, x, r, growth, *second)
     for copy in stores:
         copy.wait()
 
@@ -572,7 +575,8 @@
             dma,
             dma,
             *edges(1),
-            *edges(2),
+            *edges(1),
+            *edges(1),
             dma((7,)),
         ],
         name="bin_and_smooth",

time: 62 us -> 61.3 us (0.989)
  Pallas kernels: 60.5 us -> 59.8 us
    pallas_call x1, Pallas kernels: 59.2 us -> 58.4 us  [run(): pl.pallas_call(functools.partial(whole, rows, cols), out_shape=[pltpu.VME...]
where the time goes in v5:
time: 61.3 us; the launch traced here: 60.9 us
  Pallas kernels  59.8 us (98%)
  between operations  0.87 us (1%)
    pallas_call x1, Pallas kernels, run(): pl.pallas_call(functools.partial(whole, rows, cols), out_shape=[pltpu.VME...  58.4 us
    pallas_call x1, Pallas kernels, deliver(): pl.pallas_call(hand_over, out_shape=[jax.ShapeDtypeStruct(a.shape, a.dtyp...  1.33 us

profile of v5, /device:TPU:0, one launch (start us, length us, event | category | flops | bytes accessed | tf_op | source)
XLA Modules:
  0.0 60.9 jit_solution(13931858291928099906)
XLA Ops:
  0.6 0.0 copy-start
  0.6 58.4 %bin_and_smooth.1 = (f32[512,512]{1,0:T(8,128)S(1)}, f32[512,512]{1,0:T(8,128)S(1)}, f32[1,128]{1,0:T(1,128)S(1)}, f32[512,512]{1,0:T(8,128)}, f32[512,512]{1,0:T(8,128)}) custom-call(s32[16,128,128]{2,1,0:T(8,128)} %bitcast.7, bf16[16,128,128]{2,1,0:T(8,128)(2,1)} %bitcast.8, bf16[16,128,128]{2,1,0:T(8,128)(2,1)} %bitcast.9, s32[16,128]{1,0:T(8,128)} %bitcast.10, ...), custom_call_target="tpu_custom_call" | custom-call | tf_op jit(solution)/shard_map/bin_and_smooth/pallas_call | solution.py:550
  59.1 0.0 copy-done
  59.1 1.6 %conditional.1 = ((f32[512,512]{1,0:T(8,128)}, f32[512,512]{1,0:T(8,128)})) conditional(s32[]{:T(128)} %bitcast.4, (f32[512,512]{1,0:T(8,128)}, f32[512,512]{1,0:T(8,128)}, f32[512,512]{1,0:T(8,128)S(1)}) %tuple.43, (f32[512,512]{1,0:T(8,128)S(1)}, f32[512,512]{1,0:T(8,128)S(1)}) %tuple.15), branch_computations={%region_0.19_spmd, %region_19.20_spmd} | conditional | flops 42467336 | bytes 58017148 | solution.py:657
  59.4 1.3 %deliver.1 = (f32[512,512]{1,0:T(8,128)}, f32[512,512]{1,0:T(8,128)}) custom-call(f32[512,512]{1,0:T(8,128)S(1)} %get-tuple-element.13.refs_0_, f32[512,512]{1,0:T(8,128)S(1)} %get-tuple-element.14.refs_1_), custom_call_target="tpu_custom_call" | custom-call | tf_op jit(solution)/shard_map/cond/branch_1_fun/deliver/pallas_call | solution.py:523
Async XLA Ops:
  0.6 58.5 %copy-start = (f32[512,512]{1,0:T(8,128)S(1)}, f32[512,512]{1,0:T(8,128)}, u32[]{:S(2)}) copy-start(f32[512,512]{1,0:T(8,128)} %refs_4_.1) | copy-start | bytes 3145732

commit v6 on v5

--- a/solution.py
+++ b/solution.py
@@ -471,16 +471,16 @@
     growth_ref[...] = growth
 
     def spread(value):
-        return jnp.concatenate([jnp.broadcast_to(value, (32, WIDE))] * tiles, axis=1)
+        return jnp.concatenate([jnp.broadcast_to(value, (128, WIDE))] * tiles, axis=1)
 
     def combine(k, _):
-        at = pl.ds(k * 32, 32)
+        at = pl.ds(k * 128, 128)
         basis = [ref[at, :] for ref in (resp_ref, y1, y2, y3)]
         x_ref[at, :] = sum(spread(a * SCALE) * v for a, v in zip(xs, basis))
         r_ref[at, :] = sum(spread(a) * v for a, v in zip(rs, basis))
         return 0
 
-    lax.fori_loop(0, high // 32, combine, 0)
+    lax.fori_loop(0, high // 128, combine, 0)
     pltpu.make_async_copy(parts.at[others], parts.at[others], sent_part).wait()
 
 

time: 61.3 us -> 61.2 us (level)
  no operation moved by 1% of the time
where the time goes in v6:
time: 61.2 us; the launch traced here: 60.7 us
  Pallas kernels  59.6 us (97%)
  between operations  0.87 us (1%)
    pallas_call x1, Pallas kernels, run(): pl.pallas_call(functools.partial(whole, rows, cols), out_shape=[pltpu.VME...  58.3 us
    pallas_call x1, Pallas kernels, deliver(): pl.pallas_call(hand_over, out_shape=[jax.ShapeDtypeStruct(a.shape, a.dtyp...  1.33 us

profile of v6, /device:TPU:0, one launch (start us, length us, event | category | flops | bytes accessed | tf_op | source)
XLA Modules:
  0.0 60.7 jit_solution(4090961225075322171)
XLA Ops:
  0.6 0.0 copy-start
  0.6 58.3 %bin_and_smooth.1 = (f32[512,512]{1,0:T(8,128)S(1)}, f32[512,512]{1,0:T(8,128)S(1)}, f32[1,128]{1,0:T(1,128)S(1)}, f32[512,512]{1,0:T(8,128)}, f32[512,512]{1,0:T(8,128)}) custom-call(s32[16,128,128]{2,1,0:T(8,128)} %bitcast.7, bf16[16,128,128]{2,1,0:T(8,128)(2,1)} %bitcast.8, bf16[16,128,128]{2,1,0:T(8,128)(2,1)} %bitcast.9, s32[16,128]{1,0:T(8,128)} %bitcast.10, ...), custom_call_target="tpu_custom_call" | custom-call | tf_op jit(solution)/shard_map/bin_and_smooth/pallas_call | solution.py:550
  59.0 0.0 copy-done
  59.0 1.6 %conditional.1 = ((f32[512,512]{1,0:T(8,128)}, f32[512,512]{1,0:T(8,128)})) conditional(s32[]{:T(128)} %bitcast.4, (f32[512,512]{1,0:T(8,128)}, f32[512,512]{1,0:T(8,128)}, f32[512,512]{1,0:T(8,128)S(1)}) %tuple.43, (f32[512,512]{1,0:T(8,128)S(1)}, f32[512,512]{1,0:T(8,128)S(1)}) %tuple.15), branch_computations={%region_0.19_spmd, %region_19.20_spmd} | conditional | flops 42467336 | bytes 58017148 | solution.py:657
  59.2 1.3 %deliver.1 = (f32[512,512]{1,0:T(8,128)}, f32[512,512]{1,0:T(8,128)}) custom-call(f32[512,512]{1,0:T(8,128)S(1)} %get-tuple-element.13.refs_0_, f32[512,512]{1,0:T(8,128)S(1)} %get-tuple-element.14.refs_1_), custom_call_target="tpu_custom_call" | custom-call | tf_op jit(solution)/shard_map/cond/branch_1_fun/deliver/pallas_call | solution.py:523
Async XLA Ops:
  0.6 58.3 %copy-start = (f32[512,512]{1,0:T(8,128)S(1)}, f32[512,512]{1,0:T(8,128)}, u32[]{:S(2)}) copy-start(f32[512,512]{1,0:T(8,128)} %refs_4_.1) | copy-start | bytes 3145732
